TPU v7x, 32 devices: a whole 2x2x4 slice. The times are simulated.
32 devices in a mesh: model: 4 (over z), data: 8 (over y, x, core).
Axes of the slice: x: 2, y: 2, z: 4, core: 2. Of those that a mesh axis runs over, the one named last changes fastest.
Arguments:
- x_tokens: bfloat16 [32768, 1024], P('data')
- dy_tokens: bfloat16 [32768, 1024], P('data')
- w_col: bfloat16 [2, 1024, 1024], P(None, None, 'model')
- w_row: bfloat16 [2, 1024, 1024], P(None, 'model')
- a_old_col: float32 [2, 1024, 1024], replicated
- s_old_col: float32 [2, 1024, 256], P(None, 'model')
- a_old_row: float32 [2, 1024, 256], P(None, 'model')
- s_old_row: float32 [2, 1024, 1024], replicated
- a_inv_col: float32 [2, 1024, 1024], replicated
- s_inv_col: float32 [2, 1024, 256], P(None, 'model')
- a_inv_row: float32 [2, 1024, 256], P(None, 'model')
- s_inv_row: float32 [2, 1024, 1024], replicated
Outputs:
- output 1: float32 [2, 1024, 1024], P(None, None, 'model')
- output 2: float32 [2, 1024, 1024], P(None, 'model')
- output 3: float32 [2, 1024, 1024], replicated
- output 4: float32 [2, 1024, 256], P(None, 'model')
- output 5: float32 [2, 1024, 256], P(None, 'model')
- output 6: float32 [2, 1024, 1024], replicated
All inputs are finite; a program needn't handle non-finite values.
Results may differ from a plain program's by a relative error of at most 0.00553995.
Values are sent between devices in bfloat16 or wider.
A program may use at most 1 GiB of HBM per device.

v0:
```python
import math
import jax
import jax.numpy as jnp
from jax import lax
from jax.sharding import PartitionSpec as P

FACTOR_DECAY = 0.8
GELU_SCALE = math.sqrt(2.0 / math.pi)
GELU_CUBIC = 0.044715
EXACT = lax.Precision.HIGHEST
TN_DIMS = (((0,), (0,)), ((), ()))
NT_DIMS = (((1,), (1,)), ((), ()))


def gelu_value(pre_act):
    tanh_arg = GELU_SCALE * (pre_act + GELU_CUBIC * pre_act * pre_act * pre_act)
    return 0.5 * pre_act * (1.0 + jnp.tanh(tanh_arg))


def gelu_slope(pre_act):
    tanh_arg = GELU_SCALE * (pre_act + GELU_CUBIC * pre_act * pre_act * pre_act)
    tanh_val = jnp.tanh(tanh_arg)
    return 0.5 * (1.0 + tanh_val) + 0.5 * pre_act * (1.0 - tanh_val * tanh_val) * GELU_SCALE * (1.0 + 3.0 * GELU_CUBIC * pre_act * pre_act)


def activate(pre_act):
    return gelu_value(pre_act.astype(jnp.float32)).astype(jnp.bfloat16)


def back_gate(grad_act, pre_act):
    return (grad_act.astype(jnp.float32) * gelu_slope(pre_act.astype(jnp.float32))).astype(jnp.bfloat16)


def matmul(left_mat, right_mat):
    return jnp.dot(left_mat, right_mat, preferred_element_type=jnp.float32)


def matmul_tn(left_mat, right_mat):
    return lax.dot_general(left_mat, right_mat, TN_DIMS, preferred_element_type=jnp.float32)


def matmul_nt(left_mat, right_mat):
    return lax.dot_general(left_mat, right_mat, NT_DIMS, preferred_element_type=jnp.float32)


def exact_dot(left_mat, right_mat):
    return jnp.dot(left_mat, right_mat, precision=EXACT, preferred_element_type=jnp.float32)


def precondition(a_inv, grad_mat, s_inv):
    return exact_dot(exact_dot(a_inv, grad_mat), s_inv)


def blend_factor(old_mats, first_new, second_new, inv_rows):
    return FACTOR_DECAY * old_mats + (1.0 - FACTOR_DECAY) * inv_rows * jnp.stack([first_new, second_new])


def local_pass(x_tokens, dy_tokens, w_col, w_row):
    z_one = matmul(x_tokens, w_col[0]).astype(jnp.bfloat16)
    h_one = activate(z_one)
    z_two = lax.psum(matmul(h_one, w_row[0]), 'model').astype(jnp.bfloat16)
    h_two = activate(z_two)
    z_three = matmul(h_two, w_col[1]).astype(jnp.bfloat16)
    h_three = activate(z_three)
    g_three = back_gate(matmul_nt(dy_tokens, w_row[1]).astype(jnp.bfloat16), z_three)
    dh_two = lax.psum(matmul_nt(g_three, w_col[1]), 'model').astype(jnp.bfloat16)
    g_two = back_gate(dh_two, z_two)
    g_one = back_gate(matmul_nt(g_two, w_row[0]).astype(jnp.bfloat16), z_one)
    return [x_tokens, h_one, h_two, h_three], [g_one, g_two, g_three, dy_tokens]


def finish_step(totals, inv_rows, a_old_col, s_old_col, a_old_row, s_old_row, a_inv_col, s_inv_col, a_inv_row, s_inv_row):
    weight_grads = [total_mat * inv_rows for total_mat in totals[8:]]
    u_col = jnp.stack([precondition(a_inv_col[0], weight_grads[0], s_inv_col[0]), precondition(a_inv_col[1], weight_grads[2], s_inv_col[1])])
    u_row = jnp.stack([precondition(a_inv_row[0], weight_grads[1], s_inv_row[0]), precondition(a_inv_row[1], weight_grads[3], s_inv_row[1])])
    a_new_col = blend_factor(a_old_col, totals[0], totals[2], inv_rows)
    s_new_col = blend_factor(s_old_col, totals[4], totals[6], inv_rows)
    a_new_row = blend_factor(a_old_row, totals[1], totals[3], inv_rows)
    s_new_row = blend_factor(s_old_row, totals[5], totals[7], inv_rows)
    return (u_col, u_row, a_new_col, s_new_col, a_new_row, s_new_row)


def solution(mesh):
    data_ways = mesh.shape['data']

    def shard_body(x_tokens, dy_tokens, w_col, w_row, a_old_col, s_old_col, a_old_row, s_old_row, a_inv_col, s_inv_col, a_inv_row, s_inv_row):
        layer_in, layer_grad = local_pass(x_tokens, dy_tokens, w_col, w_row)
        local_sums = [matmul_tn(layer_in[layer], layer_in[layer]) for layer in range(4)]
        local_sums += [matmul_tn(layer_grad[layer], layer_grad[layer]) for layer in range(4)]
        local_sums += [matmul_tn(layer_in[layer], layer_grad[layer]) for layer in range(4)]
        totals = lax.psum(local_sums, 'data')
        inv_rows = 1.0 / (x_tokens.shape[0] * data_ways)
        return finish_step(totals, inv_rows, a_old_col, s_old_col, a_old_row, s_old_row, a_inv_col, s_inv_col, a_inv_row, s_inv_row)

    batch_split = P('data', None)
    col_split = P(None, None, 'model')
    row_split = P(None, 'model', None)
    replicated = P()
    return jax.shard_map(
        shard_body,
        mesh=mesh,
        in_specs=(batch_split, batch_split, col_split, row_split, replicated, row_split, row_split, replicated, replicated, row_split, row_split, replicated),
        out_specs=(col_split, row_split, replicated, row_split, row_split, replicated),
        check_vma=False,
    )
```

profile of v0, /device:TPU:0, one launch (start us, length us, event | category | flops | bytes accessed | tf_op | source)
XLA Modules:
  0.0 1586.6 jit_solution(14216338014634122411)
XLA Ops:
  7.2 5.9 convolution_convert_fusion.2
  13.1 8.5 fusion.67
  21.6 561.1 %all-reduce.6 = bf16[4096,1024]{1,0:T(8,128)(2,1)} all-reduce(f32[4096,1024]{1,0:T(8,128)} %fusion.67), channel_id=1, replica_groups=mesh['model'=4,'data'=8] {'model'}, use_global_device_ids=true, to_apply=%region_0.0 | all-reduce | flops 4194304 | bytes 25165824 | tf_op jit(solution)/shard_map/psum | solution.py:61
  582.7 7.7 fusion.2
  590.4 3.4 copy-done
  593.8 2.3 convolution_convert_fusion.1
  596.2 4.5 fusion.18
  602.1 8.1 fusion.63
  610.2 554.2 %all-reduce.7 = bf16[4096,1024]{1,0:T(8,128)(2,1)} all-reduce(f32[4096,1024]{1,0:T(8,128)} %fusion.63), channel_id=1, replica_groups=mesh['model'=4,'data'=8] {'model'}, use_global_device_ids=true, to_apply=%region_1.0 | all-reduce | flops 4194304 | bytes 25165824 | tf_op jit(solution)/shard_map/psum | solution.py:66
  1164.4 14.1 fusion.7
  1178.5 4.6 fusion.15
  1183.1 3.4 convolution_bitcast_fusion.6
  1187.9 3.8 fusion.97
  1191.7 10.9 convolution_bitcast_fusion.1
  1202.7 3.4 fusion.100
  1207.6 7.0 fusion.94
  1214.6 3.3 convolution_bitcast_fusion.7
  1217.9 10.6 convolution_bitcast_fusion.2
  1228.5 3.3 convolution_bitcast_fusion.8
  1231.8 10.5 convolution_bitcast_fusion
  1242.2 10.6 convolution_bitcast_fusion.3
  1252.9 273.2 %all-reduce.5.cloned.1.call-done = (f32[1024,256]{0,1:T(8,128)}, f32[1024,256]{0,1:T(8,128)}, f32[256,1024]{1,0:T(8,128)}, f32[256,1024]{1,0:T(8,128)}, f32[1,10...) async-done(((f32[1024,256]{0,1:T(8,128)}, ...) | async-done | bytes 22020112 | tf_op jit(solution)/shard_map/psum | solution.py:91
  1526.2 3.1 fusion.57
  1529.2 3.1 fusion.55
  1532.3 6.0 fusion.49
  1538.3 6.0 fusion.52
  1544.3 6.0 fusion.41
  1550.4 3.7 fusion.43
  1554.2 1.9 convolution_bitcast_fusion.4
  1556.0 1.9 convolution_bitcast_fusion.5
  1559.4 1.5 pad_maximum_fusion
  1562.8 16.4 %fusion.11 = (f32[2,1024,1024]{2,1,0:T(8,128)}, f32[2,1024,1024]{2,1,0:T(8,128)}) fusion(f32[1,1024,1024]{2,1,0:T(8,128)S(1)} %copy-done.1, f32[1,1024,1024]{2,1,0:T(8,128)} %get-tuple-element.11, f32[2,1024,1024]{2,1,0:T(8,128)} %param.16, f32[1,1024,1024]{2,1,0:T(8,128)} %get-tuple-element.16, f32[1,1024,1024]{2,1,0:T(8,128)} %get-tuple-element.17, ...), kind=kLoop, calls=%fused_computation.33 | loop fusion | flops 16777216 | bytes 50331648 | tf_op jit(solution)/shard_map/add | solution.py:55
  (66 shorter events, 7.9 us)
Async XLA Ops:
  7.2 5.9 copy-start.11
  7.2 1519.0 %all-reduce.5.cloned.1.call-start = ((), (), s32[]{:S(2)}) async-start(), calls=%async_computation | async-start | bytes 44040192 | tf_op jit(solution)/shard_map/psum | solution.py:91
  582.7 11.1 copy-start.10
  582.7 13.4 slice-start.6
  590.4 3.4 copy-start
  593.8 2.4 slice-start.7
  596.2 4.6 copy-start.16
  600.8 1.3 copy-start.2
  1164.4 18.7 %slice-start = ((s8[8388608]{0:T(1024)(128)(4,1)}), s8[4194304]{0:T(1024)(128)(4,1)S(1)}, s32[]{:S(2)}) async-start(s8[8388608]{0:T(1024)(128)(4,1)} %bitcast.97), calls=%async_computation.1 | async-start | bytes 8388608
  1178.5 4.6 slice-start.1
  1187.9 14.7 slice-start.4
  1191.7 10.9 slice-start.5
  1191.7 10.9 copy-start.3
  1206.0 1.6 copy-start.17
  1214.6 17.1 %slice-start.8 = ((s8[8388608]{0:T(1024)(128)(4,1)}), s8[4194304]{0:T(1024)(128)(4,1)S(1)}, s32[]{:S(2)}) async-start(s8[8388608]{0:T(1024)(128)(4,1)} %bitcast.105), calls=%async_computation.9 | async-start | bytes 8388608
  1217.9 13.9 slice-start.9
  1252.9 273.3 %copy-start.6 = (f32[2,256,256]{2,1,0:T(8,128)S(1)}, f32[2,256,256]{2,1,0:T(8,128)}, u32[]{:S(2)}) copy-start(f32[2,256,256]{2,1,0:T(8,128)} %param.22) | copy-start | bytes 1572868
  1532.3 18.1 %slice-start.2 = ((s8[8388608]{0:T(1024)(128)(4,1)}), s8[4194304]{0:T(1024)(128)(4,1)S(1)}, s32[]{:S(2)}) async-start(s8[8388608]{0:T(1024)(128)(4,1)} %bitcast.99), calls=%async_computation.3 | async-start | bytes 8388608
  1538.3 6.0 copy-start.5
  1538.3 12.1 slice-start.3
  1544.3 6.1 copy-start.4
  1550.4 3.8 copy-start.7
  1557.9 3.0 copy-start.8
  1557.9 3.0 copy-start.9
  1557.9 3.0 copy-start.12
  1558.0 3.0 copy-start.13
  1558.0 3.0 copy-start.14
  1558.0 3.0 copy-start.15
  1559.4 3.4 copy-start.1
Sparse Core Ops, SparseCore 0:
  1253.0 273.0 all-reduce.4
where the time goes:
time: 1590 us
  blocking collectives  1120 us (70%)
  waiting for transfers between devices  273 us (17%)
  matrix products  135 us (8%)
  other arithmetic  42.2 us (3%)
    psum x1, blocking collectives, local_pass(): z_two = lax.psum(matmul(h_one, w_row[0]), 'model').astype(jnp.bfloat16)  561 us
    psum x1, blocking collectives, local_pass(): lax.psum(matmul_nt(g_three, w_col[1]), 'model').astype(jnp.bfloat16)  554 us
    psum x1, waiting for transfers between devices, shard_body(): totals = lax.psum(local_sums, 'data')  273 us
    dot_general x12, matrix products, matmul_tn(): lax.dot_general(left_mat, right_mat, TN_DIMS, preferred_element_type=jnp....  69.6 us
  transfers between devices with their start and end apart: 1, of which 1 were waited for; matrix products, arithmetic and copies ran while one was open for 0% of the time, Pallas kernels for 0%

commit v1 on v0

v1 whole, which is shorter than its diff:
```python
import math
import jax
import jax.numpy as jnp
from jax import lax
from jax.sharding import PartitionSpec as P
from jax.experimental import pallas as pl
from jax.experimental.pallas import tpu as pltpu

FACTOR_DECAY = 0.8
GELU_SCALE = math.sqrt(2.0 / math.pi)
GELU_CUBIC = 0.044715
EXACT = lax.Precision.HIGHEST
TN_DIMS = (((0,), (0,)), ((), ()))
NT_DIMS = (((1,), (1,)), ((), ()))
BOTH = ('model', 'data')


def gelu_value(pre_act):
    tanh_arg = GELU_SCALE * (pre_act + GELU_CUBIC * pre_act * pre_act * pre_act)
    return 0.5 * pre_act * (1.0 + jnp.tanh(tanh_arg))


def gelu_slope(pre_act):
    tanh_arg = GELU_SCALE * (pre_act + GELU_CUBIC * pre_act * pre_act * pre_act)
    tanh_val = jnp.tanh(tanh_arg)
    return 0.5 * (1.0 + tanh_val) + 0.5 * pre_act * (1.0 - tanh_val * tanh_val) * GELU_SCALE * (1.0 + 3.0 * GELU_CUBIC * pre_act * pre_act)


def activate(pre_act):
    return gelu_value(pre_act.astype(jnp.float32)).astype(jnp.bfloat16)


def back_gate(grad_act, pre_act):
    return (grad_act.astype(jnp.float32) * gelu_slope(pre_act.astype(jnp.float32))).astype(jnp.bfloat16)


def matmul(left_mat, right_mat):
    return jnp.dot(left_mat, right_mat, preferred_element_type=jnp.float32)


def matmul_tn(left_mat, right_mat):
    return lax.dot_general(left_mat, right_mat, TN_DIMS, preferred_element_type=jnp.float32)


def matmul_nt(left_mat, right_mat):
    return lax.dot_general(left_mat, right_mat, NT_DIMS, preferred_element_type=jnp.float32)


def exact_dot(left_mat, right_mat):
    return jnp.dot(left_mat, right_mat, precision=EXACT, preferred_element_type=jnp.float32)


D_ROWS = 512
FULL_BASE = 512
BLOCK_BASE = 768
SHARE_ROWS = 896


def gram_kernel(x_ref, g1_ref, g2_ref, h1_ref, h2_ref, g3_ref, dy_ref, h3_ref, out_ref,
                act, stage, bstage, in_sem, out_sem, b_sem):
    sources = [dy_ref, h3_ref, h2_ref, g3_ref, g2_ref, h1_ref, x_ref, g1_ref]
    slots = [3, 7, 2, 6, 1, 5, 0, 4]
    loads = [pltpu.make_async_copy(src, act.at[slot], in_sem.at[slot]) for src, slot in zip(sources, slots)]
    for load in loads:
        load.start()
    started = [0]
    pend = {}

    def out_copy(slot, dst):
        return pltpu.make_async_copy(stage.at[slot], dst, out_sem.at[slot])

    for layer in (3, 2, 1, 0):
        pltpu.make_async_copy(x_ref, act.at[layer], in_sem.at[layer]).wait()
        pltpu.make_async_copy(x_ref, act.at[4 + layer], in_sem.at[4 + layer]).wait()

        def d_body(m, carry, layer=layer):
            slot = lax.rem(m, 2)
            cols = pl.ds(pl.multiple_of(m * 256, 256), 256)
            right = act[4 + layer, :, cols]
            dst = out_ref.at[pl.ds(m * 8 + 2 * layer, 2), pl.ds(0, D_ROWS)]

            if layer == 3:
                @pl.when(m >= 2)
                def _():
                    out_copy(slot, dst).wait()
                    pltpu.make_async_copy(bstage.at[slot], out_ref.at[pl.ds(0, 8), pl.ds(BLOCK_BASE, 32)], b_sem.at[slot]).wait()
            else:
                out_copy(slot, dst).wait()
                pltpu.make_async_copy(bstage.at[slot], out_ref.at[pl.ds(0, 8), pl.ds(BLOCK_BASE, 32)], b_sem.at[slot]).wait()
            prod = lax.dot_general(act[layer], right, TN_DIMS, preferred_element_type=jnp.float32)
            stage[slot] = prod.reshape(2, D_ROWS, 256)
            out_copy(slot, dst).start()
            blk = lax.dot_general(right, right, TN_DIMS, preferred_element_type=jnp.float32)
            bstage[slot] = blk.reshape(8, 32, 256)
            pltpu.make_async_copy(bstage.at[slot], out_ref.at[pl.ds(m * 8, 8), pl.ds(BLOCK_BASE + 32 * layer, 32)], b_sem.at[slot]).start()
            return carry

        lax.fori_loop(0, 4, d_body, 0)

        if layer in (2, 1):
            which = 0 if layer == 2 else 1

            def f_body(n, carry, layer=layer, which=which):
                slot = lax.rem(n, 2)
                cols = pl.ds(pl.multiple_of(n * 256, 256), 256)
                dst = out_ref.at[:, pl.ds(FULL_BASE + which * 128 + 32 * n, 32)]
                pltpu.make_async_copy(stage.at[slot], out_ref.at[pl.ds(0, 2), pl.ds(0, D_ROWS)], out_sem.at[slot]).wait()
                prod = lax.dot_general(act[layer], act[layer, :, cols], TN_DIMS, preferred_element_type=jnp.float32)
                stage[slot] = prod.reshape(2, D_ROWS, 256)
                pltpu.make_async_copy(stage.at[slot].reshape(32, 32, 256), dst, out_sem.at[slot]).start()
                return carry

            lax.fori_loop(0, 4, f_body, 0)
    for slot in range(2):
        pltpu.make_async_copy(stage.at[slot], out_ref.at[pl.ds(0, 2), pl.ds(0, D_ROWS)], out_sem.at[slot]).wait()
        pltpu.make_async_copy(bstage.at[slot], out_ref.at[pl.ds(0, 8), pl.ds(BLOCK_BASE, 32)], b_sem.at[slot]).wait()


def gram_call(x_loc, g_one, g_two, h_one, h_two, g_three, dy_loc, h_three):
    any_spec = pl.BlockSpec(memory_space=pl.ANY)
    return pl.pallas_call(
        gram_kernel,
        out_shape=jax.ShapeDtypeStruct((32, SHARE_ROWS, 256), jnp.float32),
        in_specs=[any_spec] * 8,
        out_specs=any_spec,
        scratch_shapes=[
            pltpu.VMEM((8, 1024, 1024), jnp.bfloat16),
            pltpu.VMEM((2, 2, D_ROWS, 256), jnp.float32),
            pltpu.VMEM((2, 8, 32, 256), jnp.float32),
            pltpu.SemaphoreType.DMA((8,)),
            pltpu.SemaphoreType.DMA((2,)),
            pltpu.SemaphoreType.DMA((2,)),
        ],
        compiler_params=pltpu.CompilerParams(vmem_limit_bytes=48 * 1024 * 1024),
        cost_estimate=pl.CostEstimate(flops=15_000_000_000, bytes_accessed=46_000_000, transcendentals=0),
        name='gram',
    )(x_loc, g_one, g_two, h_one, h_two, g_three, dy_loc, h_three)


def solution(mesh):
    data_ways = mesh.shape['data']
    model_ways = mesh.shape['model']
    n_dev = data_ways * model_ways

    def shard_body(x_tokens, dy_tokens, w_col, w_row, a_old_col, s_old_col, a_old_row, s_old_row, a_inv_col, s_inv_col, a_inv_row, s_inv_row):
        model_id = lax.axis_index('model')
        data_id = lax.axis_index('data')
        dev_id = model_id * data_ways + data_id
        inv_rows = 1.0 / (x_tokens.shape[0] * data_ways)
        col_part = lax.dynamic_slice(w_col, (0, 128 * data_id, 0), (2, 128, 256))
        row_part = lax.dynamic_slice(w_row, (0, 32 * data_id, 0), (2, 32, 1024))
        col_all = lax.all_gather(col_part, BOTH)
        row_all = lax.all_gather(row_part, BOTH)
        w_c = [jnp.swapaxes(col_all[:, layer].reshape(4, 1024, 256), 0, 1).reshape(1024, 1024) for layer in range(2)]
        w_r = [row_all[:, layer].reshape(1024, 1024) for layer in range(2)]
        x_cols = lax.dynamic_slice(x_tokens, (0, 256 * model_id), (x_tokens.shape[0], 256))
        dy_cols = lax.dynamic_slice(dy_tokens, (0, 256 * model_id), (x_tokens.shape[0], 256))
        ends = jnp.stack([matmul_tn(x_cols, x_tokens), matmul_tn(dy_cols, dy_tokens)]).reshape(2, 8, 32, 1024)
        ends = lax.psum_scatter(jnp.swapaxes(ends, 0, 1), 'data', scatter_dimension=0, tiled=False)
        rows_dev = x_tokens.shape[0] // model_ways
        x_loc = lax.dynamic_slice(x_tokens, (rows_dev * model_id, 0), (rows_dev, 1024))
        dy_loc = lax.dynamic_slice(dy_tokens, (rows_dev * model_id, 0), (rows_dev, 1024))
        z_one = matmul(x_loc, w_c[0]).astype(jnp.bfloat16)
        h_one = activate(z_one)
        z_two = matmul(h_one, w_r[0]).astype(jnp.bfloat16)
        h_two = activate(z_two)
        z_three = matmul(h_two, w_c[1]).astype(jnp.bfloat16)
        h_three = activate(z_three)
        g_three = back_gate(matmul_nt(dy_loc, w_r[1]).astype(jnp.bfloat16), z_three)
        g_two = back_gate(matmul_nt(g_three, w_c[1]).astype(jnp.bfloat16), z_two)
        g_one = back_gate(matmul_nt(g_two, w_r[0]).astype(jnp.bfloat16), z_one)
        parts = gram_call(x_loc, g_one, g_two, h_one, h_two, g_three, dy_loc, h_three)
        share = lax.psum_scatter(parts, BOTH, scatter_dimension=0, tiled=False)
        row_at = 32 * dev_id
        mids = jnp.swapaxes(share[FULL_BASE:BLOCK_BASE].reshape(2, 4, 32, 256), 1, 2).reshape(2, 32, 1024)
        old_a = lax.dynamic_slice(a_old_col, (0, row_at, 0), (2, 32, 1024))
        old_s = lax.dynamic_slice(s_old_row, (0, row_at, 0), (2, 32, 1024))
        keep = 1.0 - FACTOR_DECAY
        new_a = FACTOR_DECAY * old_a + keep * inv_rows * jnp.stack([ends[0], mids[0]])
        new_s = FACTOR_DECAY * old_s + keep * inv_rows * jnp.stack([mids[1], ends[1]])
        a_new_col = lax.all_gather(new_a, BOTH, axis=1, tiled=True)
        s_new_row = lax.all_gather(new_s, BOTH, axis=1, tiled=True)
        pair = [[2 * j, 2 * j + 1] for j in range(data_ways // 2)]
        grad_mat = lax.all_gather(share[:D_ROWS], 'data', axis_index_groups=pair, tiled=True) * inv_rows
        layer_id = data_id // 2
        stack_id = layer_id // 2
        is_col = lax.rem(layer_id, 2) == 0
        half_at = lax.rem(data_id, 2) * D_ROWS
        full_inv = jnp.where(is_col, lax.dynamic_slice(a_inv_col, (stack_id, half_at, 0), (1, D_ROWS, 1024))[0],
                             lax.dynamic_slice(s_inv_row, (stack_id, half_at, 0), (1, D_ROWS, 1024))[0])
        block_inv = jnp.where(is_col, lax.dynamic_slice(s_inv_col, (stack_id, 0, 0), (1, 256, 256))[0],
                              lax.dynamic_slice(a_inv_row, (stack_id, 0, 0), (1, 256, 256))[0])
        u_half = exact_dot(exact_dot(full_inv, grad_mat), block_inv)
        blk_at = 32 * data_id
        old_sc = lax.dynamic_slice(s_old_col, (0, blk_at, 0), (2, 32, 256))
        old_ar = lax.dynamic_slice(a_old_row, (0, blk_at, 0), (2, 32, 256))
        blks = share[BLOCK_BASE:].reshape(2, 2, 32, 256)
        new_sc = FACTOR_DECAY * old_sc + keep * inv_rows * blks[:, 0]
        new_ar = FACTOR_DECAY * old_ar + keep * inv_rows * blks[:, 1]
        small = jnp.concatenate([u_half, new_sc.reshape(64, 256), new_ar.reshape(64, 256)], axis=0)
        small_all = lax.all_gather(small, 'data')
        u_all = small_all[:, :D_ROWS].reshape(2, 2, 1024, 256)
        u_col = u_all[:, 0]
        u_row = jnp.swapaxes(u_all[:, 1], 1, 2)
        blk_all = jnp.swapaxes(small_all[:, D_ROWS:].reshape(8, 4, 32, 256), 0, 1).reshape(4, 256, 256)
        return (u_col, u_row, a_new_col, blk_all[:2], blk_all[2:], s_new_row)

    batch_split = P('data', None)
    col_split = P(None, None, 'model')
    row_split = P(None, 'model', None)
    replicated = P()
    return jax.shard_map(
        shard_body,
        mesh=mesh,
        in_specs=(batch_split, batch_split, col_split, row_split, replicated, row_split, row_split, replicated, replicated, row_split, row_split, replicated),
        out_specs=(col_split, row_split, replicated, row_split, row_split, replicated),
        check_vma=False,
    )
```

time: 1590 us -> 805 us (0.51)
  blocking collectives: 1120 us -> 0 us
  waiting for transfers between devices: 273 us -> 657 us
  matrix products: 135 us -> 47.9 us
  local copies, waits for them, and re-layouts: 5.73 us -> 49.4 us
  other arithmetic: 42.2 us -> 6.78 us
  Pallas kernels: 0 us -> 26.7 us
    psum x2 -> x0, blocking collectives: 1120 us -> none  [the longest x1 561 us: local_pass(): z_two = lax.psum(matmul(h_one, w_row[0]), 'model').astype(jnp.bfloat16)]
    reduce_scatter x0 -> x2, waiting for transfers between devices: none -> 349 us  [the longest x1 309 us: shard_body(): share = lax.psum_scatter(parts, BOTH, scatter_dimension=0, tiled=False)]
    all_gather x0 -> x6, waiting for transfers between devices: none -> 307 us  [the longest x1 79.9 us: shard_body(): s_new_row = lax.all_gather(new_s, BOTH, axis=1, tiled=True)]
    psum x1 -> x0, waiting for transfers between devices: 273 us -> none  [shard_body(): totals = lax.psum(local_sums, 'data')]
    dot_general x12 -> x2, matrix products: 69.6 us -> 12.8 us  [matmul_tn(): lax.dot_general(left_mat, right_mat, TN_DIMS, preferred_element_type=jnp....]
    pallas_call x0 -> x1, Pallas kernels: none -> 26.7 us  [gram_call(): pl.pallas_call(gram_kernel, out_shape=jax.ShapeDtypeStruct((32, SHARE_ROW...]
    dot_general x8 -> x2, matrix products: 31.6 us -> 4.91 us  [exact_dot(): jnp.dot(left_mat, right_mat, precision=EXACT, preferred_element_type=jnp....]
    convert_element_type x2 -> x0, other arithmetic: 21.7 us -> none  [the longest x1 14.1 us: back_gate(): (grad_act.astype(jnp.float32) * gelu_slope(pre_act.astype(jnp.float32)))....]
  transfers between devices with their start and end apart: 1 -> 8, of which waited for: 1 -> 8; matrix products, arithmetic and copies ran while one was open for 0% -> 6% of each run, Pallas kernels for 0% -> 0%
where the time goes in v1:
time: 805 us; the launch traced here: 804 us
  waiting for transfers between devices  657 us (82%)
  local copies, waits for them, and re-layouts  49.4 us (6%)
  matrix products  47.9 us (6%)
  Pallas kernels  26.7 us (3%)
  between operations  15.8 us (2%)
    reduce_scatter x1, waiting for transfers between devices, shard_body(): share = lax.psum_scatter(parts, BOTH, scatter_dimension=0, tiled=False)  309 us
    all_gather x1, waiting for transfers between devices, shard_body(): s_new_row = lax.all_gather(new_s, BOTH, axis=1, tiled=True)  79.9 us
    all_gather x1, waiting for transfers between devices, shard_body(): a_new_col = lax.all_gather(new_a, BOTH, axis=1, tiled=True)  71.4 us
    all_gather x1, waiting for transfers between devices, shard_body(): col_all = lax.all_gather(col_part, BOTH)  61.5 us
    all_gather x1, waiting for transfers between devices, shard_body(): row_all = lax.all_gather(row_part, BOTH)  55.3 us
    reduce_scatter x1, waiting for transfers between devices, shard_body(): lax.psum_scatter(jnp.swapaxes(ends, 0, 1), 'data', scatter_dimension=0, t...  40.4 us
    all_gather x1, waiting for transfers between devices, shard_body(): small_all = lax.all_gather(small, 'data')  38.4 us
    pallas_call x1, Pallas kernels, gram_call(): pl.pallas_call(gram_kernel, out_shape=jax.ShapeDtypeStruct((32, SHARE_ROW...  26.7 us
  transfers between devices with their start and end apart: 8, of which 8 were waited for; matrix products, arithmetic and copies ran while one was open for 6% of the time, Pallas kernels for 0%

profile of v1, /device:TPU:0, one launch (start us, length us, event | category | flops | bytes accessed | tf_op | source)
XLA Modules:
  0.0 804.1 jit_solution(8720663944060399691)
XLA Ops:
  10.0 1.6 constant_dynamic-slice_fusion.1
  11.6 4.0 constant_dynamic-slice_fusion.2
  15.6 61.5 %all-gather.17.cloned.1.call-done = bf16[64,128,256]{2,1,0:T(8,128)(2,1)} async-done(((bf16[2,128,256]{2,1,0:T(8,128)(2,1)}), bf16[64,128,256]{2,1,0:T(8,128)(2,1)}) %all-gather.17.cloned.1.call-update) | async-done | bytes 4194320 | tf_op jit(solution)/shard_map/all_gather | solution.py:152
  77.1 4.7 fusion.68
  81.8 3.9 copy.56
  85.8 55.3 %all-gather.15.cloned.1.call-done = bf16[64,32,1024]{2,1,0:T(8,128)(2,1)} async-done(((bf16[2,32,1024]{2,1,0:T(8,128)(2,1)}), bf16[64,32,1024]{2,1,0:T(8,128)(2,1)}) %all-gather.15.cloned.1.call-update) | async-done | bytes 4194320 | tf_op jit(solution)/shard_map/all_gather | solution.py:153
  141.1 5.1 fusion.67
  146.2 4.0 copy.57
  150.2 6.2 fusion.18
  156.3 4.9 fusion.12
  161.2 4.9 fusion.11
  166.2 4.7 fusion.10.g3_ref
  170.9 4.6 fusion.17.g2_ref
  175.5 4.9 fusion.23.g1_ref
  180.4 26.7 %gram.1 = f32[32,896,256]{2,1,0:T(8,128)} custom-call(bf16[1024,1024]{1,0:T(8,128)(2,1)S(1)} %get-tuple-element.51.x_ref, bf16[1024,1024]{1,0:T(8,128)(2,1)S(1)} %fusion.23.g1_ref, bf16[1024,1024]{1,0:T(8,128)(2,1)} %copy-done.10, bf16[1024,1024]{1,0:T(8,128)(2,1)} %get-tuple-element.44.h1_ref, bf16[1024,1024]{1,0:T(8,128)(2,1)} %get-tuple-element.46.h2_ref, ...), custom_call_target="tpu_custom_call" | custom-call | flops 15000000512 | bytes 46000000 | tf_op jit(solution)/shard_map/gram/pallas_call | solution.py:121
  207.2 309.1 %reduce-scatter.3.cloned.1.call-done = f32[1,896,256]{2,1,0:T(8,128)} async-done(((f32[32,896,256]{2,1,0:T(8,128)}), f32[1,896,256]{2,1,0:T(8,128)}) %reduce-scatter.3.cloned.1.call-update) | async-done | bytes 917520 | tf_op jit(solution)/shard_map/reduce_scatter | solution.py:173
  516.3 1.9 slice.110
  518.2 6.4 fusion.37
  524.6 6.4 fusion.35
  531.0 1.6 maximum_bitcast_fusion
  534.8 4.3 fusion.33
  540.7 40.4 %reduce-scatter.5.cloned.1.call-done = f32[1,2,32,1024]{3,2,1,0:T(8,128)} async-done(((f32[8,2,32,1024]{3,2,1,0:T(8,128)}), f32[1,2,32,1024]{3,2,1,0:T(8,128)}) %reduce-scatter.5.cloned.1.call-update) | async-done | bytes 262160 | tf_op jit(solution)/shard_map/reduce_scatter | solution.py:159
  582.1 1.7 fusion.46
  583.9 1.7 fusion.47
  585.7 38.4 %all-gather.21.cloned.1.call-done = f32[5120,256]{1,0:T(8,128)} async-done(((f32[640,256]{1,0:T(8,128)}), f32[5120,256]{1,0:T(8,128)}) %all-gather.21.cloned.1.call-update) | async-done | bytes 5242896 | tf_op jit(solution)/shard_map/all_gather | solution.py:201
  624.1 2.6 slice.114
  628.0 1.7 slice_bitcast_fusion
  629.8 1.8 copy.66
  633.4 71.4 %all-gather.11.cloned.1.call-done = f32[2,1024,1024]{2,1,0:T(8,128)} async-done(((f32[2,32,1024]{2,1,0:T(8,128)}), f32[2,1024,1024]{2,1,0:T(8,128)}) %all-gather.11.cloned.1.call-update) | async-done | bytes 8388624 | tf_op jit(solution)/shard_map/all_gather | solution.py:181
  704.8 79.9 %all-gather.13.cloned.1.call-done = f32[2,1024,1024]{2,1,0:T(8,128)} async-done(((f32[2,32,1024]{2,1,0:T(8,128)}), f32[2,1024,1024]{2,1,0:T(8,128)}) %all-gather.13.cloned.1.call-update) | async-done | bytes 8388624 | tf_op jit(solution)/shard_map/all_gather | solution.py:182
  784.7 8.6 %copy.73 = f32[2,1024,1024]{2,1,0:T(8,128)} copy(f32[2,1024,1024]{2,1,0:T(8,128)} %all-gather.11.cloned.1.call-done) | data formatting | bytes 16777216
  793.3 3.4 copy.74
  (55 shorter events, 9.9 us)
Async XLA Ops:
  8.0 1.2 copy-start
  8.0 69.1 %all-gather.17.cloned.1.call-start = ((), (), s32[]{:S(2)}) async-start(), calls=%async_computation.7 | async-start | bytes 4325376 | tf_op jit(solution)/shard_map/all_gather | solution.py:152
  9.9 131.1 %all-gather.15.cloned.1.call-start = ((), (), s32[]{:S(2)}) async-start(), calls=%async_computation.6 | async-start | bytes 4325376 | tf_op jit(solution)/shard_map/all_gather | solution.py:153
  11.6 504.7 %reduce-scatter.3.cloned.1.call-start = ((), (), s32[]{:S(2)}) async-start(), calls=%async_computation.2 | async-start | bytes 30277632 | tf_op jit(solution)/shard_map/reduce_scatter | solution.py:173
  150.2 6.2 copy-start.5
  156.3 4.9 copy-start.3
  161.2 4.9 copy-start.4
  161.2 4.9 copy-start.6
  170.9 4.7 copy-start.9
  175.5 4.9 copy-start.10
  207.2 327.6 %all-gather.19.cloned.1.call-start = ((), (), s32[]{:S(2)}) async-start(), calls=%async_computation.8 | async-start | bytes 1572864 | tf_op jit(solution)/shard_map/all_gather | solution.py:184
  518.2 62.9 %reduce-scatter.5.cloned.1.call-start = ((), (), s32[]{:S(2)}) async-start(), calls=%async_computation.3 | async-start | bytes 2359296 | tf_op jit(solution)/shard_map/reduce_scatter | solution.py:159
  531.0 1.9 slice-start
  532.6 6.5 copy-start.7
  532.6 6.5 copy-start.8
  532.6 91.4 %all-gather.21.cloned.1.call-start = ((), (), s32[]{:S(2)}) async-start(), calls=%async_computation.9 | async-start | bytes 5898240 | tf_op jit(solution)/shard_map/all_gather | solution.py:201
  533.9 48.2 %slice-start.1 = ((f32[1,896,256]{2,1,0:T(8,128)}), f32[1,256,256]{2,1,0:T(8,128)S(1)}, s32[]{:S(2)}) async-start(f32[1,896,256]{2,1,0:T(8,128)} %reduce-scatter.3.cloned.1.call-done), calls=%async_computation.11 | async-start | bytes 524288 | tf_op jit(solution)/shard_map/slice | solution.py:175
  540.6 164.2 %all-gather.11.cloned.1.call-start = ((), (), s32[]{:S(2)}) async-start(), calls=%async_computation.4 | async-start | bytes 8650752 | tf_op jit(solution)/shard_map/all_gather | solution.py:181
  583.9 200.9 %all-gather.13.cloned.1.call-start = ((), (), s32[]{:S(2)}) async-start(), calls=%async_computation.5 | async-start | bytes 8650752 | tf_op jit(solution)/shard_map/all_gather | solution.py:182
  784.7 8.6 %copy-start.2 = (f32[2,1024,1024]{2,1,0:T(8,128)S(1)}, f32[2,1024,1024]{2,1,0:T(8,128)}, u32[]{:S(2)}) copy-start(f32[2,1024,1024]{2,1,0:T(8,128)} %all-gather.13.cloned.1.call-done) | copy-start | bytes 25165828
  793.3 3.4 copy-start.1
Sparse Core Ops, SparseCore 0:
  12.3 64.8 all-gather.16
  80.5 60.4 all-gather.14
  207.3 308.9 reduce-scatter.2
  518.3 16.4 all-gather.18
Sparse Core Ops, SparseCore 1:
  532.7 48.3 reduce-scatter.4
  583.4 40.6 all-gather.20
  627.5 77.3 all-gather.10
  708.4 76.3 all-gather.12

commit v2 on v1

--- a/solution.py
+++ b/solution.py
@@ -1,3 +1,4 @@
+import functools
 import math
 import jax
 import jax.numpy as jnp
@@ -137,6 +138,357 @@
     )(x_loc, g_one, g_two, h_one, h_two, g_three, dy_loc, h_three)
 
 
+MESH_ID = pl.DeviceIdType.MESH
+CHUNK_ORDER = ((0, 0), (3, 0), (0, 1), (3, 1), (1, 0), (2, 0), (1, 1), (2, 1))
+
+
+def torus_place():
+    z = lax.axis_index('model')
+    d = lax.axis_index('data')
+    y = d // 4
+    x = (d // 2) % 2
+    c = d % 2
+    near = {'x': (z, d + 2 - 4 * x), 'y': (z, d + 4 - 8 * y), 'c': (z, d + 1 - 2 * c), 'up': (z + 1, d), 'dn': (z - 1, d)}
+    return z, y, x, c, near
+
+
+def meet_neighbours(z, near):
+    barrier = pltpu.get_barrier_semaphore()
+    for side in ('x', 'y', 'c'):
+        pl.semaphore_signal(barrier, inc=1, device_id=near[side], device_id_type=MESH_ID)
+
+    @pl.when(z < 3)
+    def _():
+        pl.semaphore_signal(barrier, inc=1, device_id=near['up'], device_id_type=MESH_ID)
+
+    @pl.when(z > 0)
+    def _():
+        pl.semaphore_signal(barrier, inc=1, device_id=near['dn'], device_id_type=MESH_ID)
+    pl.semaphore_wait(barrier, 3 + (z + 3) // 4 + (6 - z) // 4)
+
+
+def remote(src, dst, send_sem, recv_sem, where):
+    return pltpu.make_async_remote_copy(src_ref=src, dst_ref=dst, send_sem=send_sem, recv_sem=recv_sem, device_id=where, device_id_type=MESH_ID)
+
+
+def gather_kernel(n_plane, *refs):
+    if n_plane:
+        piece_ref, plane_ref, out_ref, pout_ref = refs[:4]
+        sems = refs[4:]
+    else:
+        piece_ref, out_ref = refs[:2]
+        sems = refs[2:]
+    load_sem, z_recv, x_recv, y_recv, d_recv, c_recv, up_send, dn_send, x_send, y_send, dy_send, dx_send, c_send = sems
+    z, y, x, c, near = torus_place()
+    half = piece_ref.shape[0] // 2
+    load = pltpu.make_async_copy(piece_ref, out_ref.at[z, y, x, c], load_sem.at[0])
+    load.start()
+    if n_plane:
+        pload = pltpu.make_async_copy(plane_ref, pout_ref.at[y, x, c], load_sem.at[1])
+        pload.start()
+        phalf = plane_ref.shape[0] // 2
+    meet_neighbours(z, near)
+
+    def view(zs, yy, xx, cc):
+        return pout_ref.at[yy, xx, cc] if zs is None else out_ref.at[zs, yy, xx, cc]
+
+    def part(zs, yy, xx, cc, which):
+        size = phalf if zs is None else half
+        return view(zs, yy, xx, cc).at[pl.ds(which * size, size)]
+
+    def at(zs):
+        return 4 if zs is None else zs
+
+    def x_copy(zs):
+        return remote(view(zs, y, x, c), view(zs, y, x, c), x_send.at[at(zs)], x_recv.at[at(zs)], near['x'])
+
+    def y_copy(zs):
+        return remote(view(zs, y, x, c), view(zs, y, x, c), y_send.at[at(zs)], y_recv.at[at(zs)], near['y'])
+
+    def dy_copy(zs):
+        return remote(part(zs, y, 1 - x, c, 0), part(zs, y, 1 - x, c, 0), dy_send.at[at(zs)], d_recv.at[at(zs), 0], near['y'])
+
+    def dx_copy(zs):
+        return remote(part(zs, 1 - y, x, c, 1), part(zs, 1 - y, x, c, 1), dx_send.at[at(zs)], d_recv.at[at(zs), 1], near['x'])
+
+    def c_copy(zs, kind):
+        yy = y if kind in (0, 1) else 1 - y
+        xx = x if kind in (0, 2) else 1 - x
+        return remote(view(zs, yy, xx, c), view(zs, yy, xx, c), c_send.at[at(zs), kind], c_recv.at[at(zs), kind], near['c'])
+
+    def up_copy(zs):
+        return remote(view(zs, y, x, c), view(zs, y, x, c), up_send.at[at(zs)], z_recv.at[at(zs)], near['up'])
+
+    def dn_copy(zs):
+        return remote(view(zs, y, x, c), view(zs, y, x, c), dn_send.at[at(zs)], z_recv.at[at(zs)], near['dn'])
+
+    def guard(off, body):
+        if off is None:
+            body(None)
+        elif off == 0:
+            body(z)
+        elif off < 0:
+            pl.when(z >= -off)(lambda: body(z + off))
+        else:
+            pl.when(z <= 3 - off)(lambda: body(z + off))
+
+    def z_step(off):
+        def body(zs):
+            if off is None:
+                pload.wait()
+            elif off == 0:
+                load.wait()
+            else:
+                up_copy(zs).wait_recv()
+            if off is not None and off <= 0:
+                pl.when(z < 3)(lambda: up_copy(zs).start())
+            if off is not None and off >= 0:
+                pl.when(z > 0)(lambda: dn_copy(zs).start())
+            x_copy(zs).start()
+            y_copy(zs).start()
+            c_copy(zs, 0).start()
+        guard(off, body)
+
+    def xy_step(off):
+        def body(zs):
+            remote(view(zs, y, 1 - x, c), view(zs, y, 1 - x, c), x_send.at[at(zs)], x_recv.at[at(zs)], near['x']).wait_recv()
+            dy_copy(zs).start()
+            c_copy(zs, 1).start()
+            remote(view(zs, 1 - y, x, c), view(zs, 1 - y, x, c), y_send.at[at(zs)], y_recv.at[at(zs)], near['y']).wait_recv()
+            dx_copy(zs).start()
+            c_copy(zs, 2).start()
+        guard(off, body)
+
+    def diag_step(off):
+        def body(zs):
+            for which in range(2):
+                remote(part(zs, 1 - y, 1 - x, c, which), part(zs, 1 - y, 1 - x, c, which), dy_send.at[at(zs)], d_recv.at[at(zs), which], near['y']).wait_recv()
+            c_copy(zs, 3).start()
+        guard(off, body)
+
+    def last_step(off):
+        def body(zs):
+            for kind in range(4):
+                yy = y if kind in (0, 1) else 1 - y
+                xx = x if kind in (0, 2) else 1 - x
+                remote(view(zs, yy, xx, 1 - c), view(zs, yy, xx, 1 - c), c_send.at[at(zs), kind], c_recv.at[at(zs), kind], near['c']).wait_recv()
+                c_copy(zs, kind).wait_send()
+            x_copy(zs).wait_send()
+            y_copy(zs).wait_send()
+            dy_copy(zs).wait_send()
+            dx_copy(zs).wait_send()
+            if off is not None and off <= 0:
+                pl.when(z < 3)(lambda: up_copy(zs).wait_send())
+            if off is not None and off >= 0:
+                pl.when(z > 0)(lambda: dn_copy(zs).wait_send())
+        guard(off, body)
+
+    lead = [None] if n_plane else []
+    waves = [lead + [0], [-1, 1], [-2, 2], [-3, 3]]
+    for step in range(6):
+        for func, lag in ((z_step, 0), (xy_step, 1), (diag_step, 2)):
+            if 0 <= step - lag < 4:
+                for off in waves[step - lag]:
+                    func(off)
+    for wave in waves:
+        for off in wave:
+            last_step(off)
+
+
+def gather_call(piece, plane, collective_id, name):
+    dtype = piece.dtype
+    out_shape = [jax.ShapeDtypeStruct((4, 2, 2, 2) + piece.shape, dtype)]
+    args = [piece]
+    if plane is not None:
+        out_shape.append(jax.ShapeDtypeStruct((2, 2, 2) + plane.shape, plane.dtype))
+        args.append(plane)
+    dma = pltpu.SemaphoreType.DMA
+    size = sum(math_prod(o.shape) * o.dtype.itemsize for o in out_shape)
+    out = pl.pallas_call(
+        functools.partial(gather_kernel, 0 if plane is None else 1),
+        out_shape=out_shape,
+        in_specs=[pl.BlockSpec(memory_space=pltpu.HBM)] * len(args),
+        out_specs=[pl.BlockSpec(memory_space=pltpu.VMEM)] * len(out_shape),
+        scratch_shapes=[dma((2,)), dma((5,)), dma((5,)), dma((5,)), dma((5, 2)), dma((5, 4)), dma((5,)), dma((5,)), dma((5,)), dma((5,)), dma((5,)), dma((5,)), dma((5, 4))],
+        compiler_params=pltpu.CompilerParams(collective_id=collective_id, has_side_effects=True, vmem_limit_bytes=size + 8 * 1024 * 1024),
+        cost_estimate=pl.CostEstimate(flops=50_000_000_000, bytes_accessed=size, transcendentals=0),
+        name=name,
+    )(*args)
+    return out
+
+
+def math_prod(shape):
+    n = 1
+    for s in shape:
+        n *= s
+    return n
+
+
+def add_into(dst, src, rows):
+    step = 32 if rows % 32 == 0 else 16 if rows % 16 == 0 else 8
+
+    def body(i, carry):
+        span = pl.ds(pl.multiple_of(i * step, 8), step)
+        dst[span, :] = dst[span, :] + src[span, :]
+        return carry
+
+    lax.fori_loop(0, rows // step, body, 0)
+
+
+def scatter_kernel(rows, parts_ref, share_ref, own, mate, one_x, one_y, two_x, two_y, up_buf, dn_buf,
+                   own_sem, mate_send, mate_recv, x1_send, x1_recv, y1_send, y1_recv, x2_send, x2_recv, y2_send, y2_recv,
+                   up_send, up_recv, dn_send, dn_recv, out_sem):
+    z, y, x, c, near = torus_place()
+    sub = rows // 4
+    loads = {}
+    for k, (zd, h) in enumerate(CHUNK_ORDER):
+        loads[k] = []
+        for col in range(2):
+            span = pl.ds(col * 2 * sub + h * sub, sub)
+            load = pltpu.make_async_copy(parts_ref.at[zd, :, :, c, span], own.at[zd, :, :, span], own_sem.at[k, col])
+            load.start()
+            loads[k].append(load)
+    meet_neighbours(z, near)
+    mates = {}
+    for k, (zd, h) in enumerate(CHUNK_ORDER):
+        mates[k] = []
+        for col in range(2):
+            span = pl.ds(col * 2 * sub + h * sub, sub)
+            copy = remote(parts_ref.at[zd, :, :, 1 - c, span], mate.at[zd, :, :, span], mate_send.at[k, col], mate_recv.at[k, col], near['c'])
+            copy.start()
+            mates[k].append(copy)
+
+    def spans(h):
+        return pl.ds(h * sub, sub), pl.ds(2 * sub + h * sub, sub)
+
+    def one_copies(k):
+        zd, h = CHUNK_ORDER[k]
+        first, second = spans(h)
+        piece = pl.ds(h * sub, sub)
+        return (remote(own.at[zd, :, 1 - x, first], one_x.at[zd, :, piece], x1_send.at[k], x1_recv.at[k], near['x']),
+                remote(own.at[zd, 1 - y, :, second], one_y.at[zd, :, piece], y1_send.at[k], y1_recv.at[k], near['y']))
+
+    def two_copies(k):
+        zd, h = CHUNK_ORDER[k]
+        first, second = spans(h)
+        piece = pl.ds(h * sub, sub)
+        return (remote(own.at[zd, 1 - y, x, first], two_y.at[zd, piece], y2_send.at[k], y2_recv.at[k], near['y']),
+                remote(own.at[zd, y, 1 - x, second], two_x.at[zd, piece], x2_send.at[k], x2_recv.at[k], near['x']))
+
+    def z_copies(k):
+        zd, h = CHUNK_ORDER[k]
+        out = []
+        for col, span in enumerate(spans(h)):
+            out.append((remote(own.at[zd, y, x, span], up_buf.at[zd, span], dn_send.at[k, col], up_recv.at[k, col], near['dn']),
+                        remote(own.at[zd, y, x, span], dn_buf.at[zd, span], up_send.at[k, col], dn_recv.at[k, col], near['up'])))
+        return out
+
+    def step_a(k):
+        zd, h = CHUNK_ORDER[k]
+        first, second = spans(h)
+        ones = one_copies(k)
+        loads[k][0].wait()
+        mates[k][0].wait_recv()
+        for yy in range(2):
+            add_into(own.at[zd, yy, 1 - x, first], mate.at[zd, yy, 1 - x, first], sub)
+        ones[0].start()
+        loads[k][1].wait()
+        mates[k][1].wait_recv()
+        for xx in range(2):
+            add_into(own.at[zd, 1 - y, xx, second], mate.at[zd, 1 - y, xx, second], sub)
+        ones[1].start()
+        for yy in range(2):
+            add_into(own.at[zd, yy, x, first], mate.at[zd, yy, x, first], sub)
+        for xx in range(2):
+            add_into(own.at[zd, y, xx, second], mate.at[zd, y, xx, second], sub)
+
+    def step_b(k):
+        zd, h = CHUNK_ORDER[k]
+        first, second = spans(h)
+        piece = pl.ds(h * sub, sub)
+        ones, twos = one_copies(k), two_copies(k)
+        ones[0].wait_recv()
+        add_into(own.at[zd, 1 - y, x, first], one_x.at[zd, 1 - y, piece], sub)
+        twos[0].start()
+        ones[1].wait_recv()
+        add_into(own.at[zd, y, 1 - x, second], one_y.at[zd, 1 - x, piece], sub)
+        twos[1].start()
+        add_into(own.at[zd, y, x, first], one_x.at[zd, y, piece], sub)
+        add_into(own.at[zd, y, x, second], one_y.at[zd, x, piece], sub)
+
+    def step_c(k):
+        zd, h = CHUNK_ORDER[k]
+        first, second = spans(h)
+        piece = pl.ds(h * sub, sub)
+        twos = two_copies(k)
+        zcs = z_copies(k)
+        for col, (copy, buf, span) in enumerate(((twos[0], two_y, first), (twos[1], two_x, second))):
+            copy.wait_recv()
+            add_into(own.at[zd, y, x, span], buf.at[zd, piece], sub)
+
+            @pl.when((z < 3) & (z >= zd))
+            def _(col=col, span=span):
+                zcs[col][0].wait_recv()
+                add_into(own.at[zd, y, x, span], up_buf.at[zd, span], sub)
+
+            @pl.when((z > 0) & (z <= zd))
+            def _(col=col, span=span):
+                zcs[col][1].wait_recv()
+                add_into(own.at[zd, y, x, span], dn_buf.at[zd, span], sub)
+            pl.when(z > zd)(lambda: zcs[col][0].start())
+            pl.when(z < zd)(lambda: zcs[col][1].start())
+
+            @pl.when(z == zd)
+            def _(col=col, span=span):
+                pltpu.make_async_copy(own.at[zd, y, x, span], share_ref.at[span], out_sem.at[h, col]).start()
+
+    n = len(CHUNK_ORDER)
+    for step in range(n + 3):
+        if step < n:
+            step_a(step)
+        if 0 <= step - 1 < n:
+            step_b(step - 1)
+        if 0 <= step - 3 < n:
+            step_c(step - 3)
+    for k, (zd, h) in enumerate(CHUNK_ORDER):
+        for copy in mates[k] + list(one_copies(k)) + list(two_copies(k)):
+            copy.wait_send()
+        for col, (down, up) in enumerate(z_copies(k)):
+            pl.when(z > zd)(lambda: down.wait_send())
+            pl.when(z < zd)(lambda: up.wait_send())
+    for h in range(2):
+        for col in range(2):
+            span = spans(h)[col]
+            pltpu.make_async_copy(own.at[0, y, x, span], share_ref.at[span], out_sem.at[h, col]).wait()
+
+
+def scatter_call(parts, collective_id, name):
+    rows = parts.shape[-2]
+    half = rows // 2
+    f32 = jnp.float32
+    dma = pltpu.SemaphoreType.DMA
+    n = len(CHUNK_ORDER)
+    one = (n,)
+    two = (n, 2)
+    return pl.pallas_call(
+        functools.partial(scatter_kernel, rows),
+        out_shape=jax.ShapeDtypeStruct((rows, 256), f32),
+        in_specs=[pl.BlockSpec(memory_space=pltpu.HBM)],
+        out_specs=pl.BlockSpec(memory_space=pltpu.HBM),
+        scratch_shapes=[
+            pltpu.VMEM((4, 2, 2, rows, 256), f32), pltpu.VMEM((4, 2, 2, rows, 256), f32),
+            pltpu.VMEM((4, 2, half, 256), f32), pltpu.VMEM((4, 2, half, 256), f32),
+            pltpu.VMEM((4, half, 256), f32), pltpu.VMEM((4, half, 256), f32),
+            pltpu.VMEM((4, rows, 256), f32), pltpu.VMEM((4, rows, 256), f32),
+            dma(two), dma(two), dma(two), dma(one), dma(one), dma(one), dma(one), dma(one), dma(one), dma(one), dma(one),
+            dma(two), dma(two), dma(two), dma(two), dma((2, 2)),
+        ],
+        compiler_params=pltpu.CompilerParams(collective_id=collective_id, has_side_effects=True, vmem_limit_bytes=60 * 1024 * 1024),
+        cost_estimate=pl.CostEstimate(flops=120_000_000_000, bytes_accessed=60_000_000, transcendentals=0),
+        name=name,
+    )(parts.reshape(4, 2, 2, 2, rows, 256))
+
+
 def solution(mesh):
     data_ways = mesh.shape['data']
     model_ways = mesh.shape['model']
@@ -149,10 +501,11 @@
         inv_rows = 1.0 / (x_tokens.shape[0] * data_ways)
         col_part = lax.dynamic_slice(w_col, (0, 128 * data_id, 0), (2, 128, 256))
         row_part = lax.dynamic_slice(w_row, (0, 32 * data_id, 0), (2, 32, 1024))
-        col_all = lax.all_gather(col_part, BOTH)
-        row_all = lax.all_gather(row_part, BOTH)
-        w_c = [jnp.swapaxes(col_all[:, layer].reshape(4, 1024, 256), 0, 1).reshape(1024, 1024) for layer in range(2)]
-        w_r = [row_all[:, layer].reshape(1024, 1024) for layer in range(2)]
+        row_part = jnp.swapaxes(row_part.reshape(2, 32, 4, 256), 1, 2).reshape(256, 256)
+        (w_all,) = gather_call(jnp.concatenate([col_part.reshape(256, 256), row_part], axis=0), None, 1, 'weights')
+        w_all = w_all.reshape(4, 8, 4, 128, 256)
+        w_c = [jnp.transpose(w_all[:, :, layer].reshape(4, 1024, 256), (1, 0, 2)).reshape(1024, 1024) for layer in range(2)]
+        w_r = [jnp.swapaxes(w_all[:, :, 2 + layer].reshape(32, 4, 32, 256), 1, 2).reshape(1024, 1024) for layer in range(2)]
         x_cols = lax.dynamic_slice(x_tokens, (0, 256 * model_id), (x_tokens.shape[0], 256))
         dy_cols = lax.dynamic_slice(dy_tokens, (0, 256 * model_id), (x_tokens.shape[0], 256))
         ends = jnp.stack([matmul_tn(x_cols, x_tokens), matmul_tn(dy_cols, dy_tokens)]).reshape(2, 8, 32, 1024)
@@ -170,7 +523,7 @@
         g_two = back_gate(matmul_nt(g_three, w_c[1]).astype(jnp.bfloat16), z_two)
         g_one = back_gate(matmul_nt(g_two, w_r[0]).astype(jnp.bfloat16), z_one)
         parts = gram_call(x_loc, g_one, g_two, h_one, h_two, g_three, dy_loc, h_three)
-        share = lax.psum_scatter(parts, BOTH, scatter_dimension=0, tiled=False)
+        share = scatter_call(parts, 2, 'sums')
         row_at = 32 * dev_id
         mids = jnp.swapaxes(share[FULL_BASE:BLOCK_BASE].reshape(2, 4, 32, 256), 1, 2).reshape(2, 32, 1024)
         old_a = lax.dynamic_slice(a_old_col, (0, row_at, 0), (2, 32, 1024))
@@ -178,8 +531,6 @@
         keep = 1.0 - FACTOR_DECAY
         new_a = FACTOR_DECAY * old_a + keep * inv_rows * jnp.stack([ends[0], mids[0]])
         new_s = FACTOR_DECAY * old_s + keep * inv_rows * jnp.stack([mids[1], ends[1]])
-        a_new_col = lax.all_gather(new_a, BOTH, axis=1, tiled=True)
-        s_new_row = lax.all_gather(new_s, BOTH, axis=1, tiled=True)
         pair = [[2 * j, 2 * j + 1] for j in range(data_ways // 2)]
         grad_mat = lax.all_gather(share[:D_ROWS], 'data', axis_index_groups=pair, tiled=True) * inv_rows
         layer_id = data_id // 2
@@ -198,7 +549,10 @@
         new_sc = FACTOR_DECAY * old_sc + keep * inv_rows * blks[:, 0]
         new_ar = FACTOR_DECAY * old_ar + keep * inv_rows * blks[:, 1]
         small = jnp.concatenate([u_half, new_sc.reshape(64, 256), new_ar.reshape(64, 256)], axis=0)
-        small_all = lax.all_gather(small, 'data')
+        fact_all, small_all = gather_call(jnp.concatenate([new_a, new_s], axis=0).reshape(128, 1024), small, 3, 'results')
+        fact_all = jnp.swapaxes(fact_all.reshape(32, 4, 32, 1024), 0, 1).reshape(4, 1024, 1024)
+        a_new_col, s_new_row = fact_all[:2], fact_all[2:]
+        small_all = small_all.reshape(8, 640, 256)
         u_all = small_all[:, :D_ROWS].reshape(2, 2, 1024, 256)
         u_col = u_all[:, 0]
         u_row = jnp.swapaxes(u_all[:, 1], 1, 2)

time: 805 us -> 502 us (0.62)
  waiting for transfers between devices: 657 us -> 52.4 us
  Pallas kernels: 26.7 us -> 322 us
    reduce_scatter x1 -> x0, waiting for transfers between devices: 309 us -> none  [shard_body(): share = lax.psum_scatter(parts, BOTH, scatter_dimension=0, tiled=False)]
    all_gather x5 -> x0, waiting for transfers between devices: 307 us -> none  [the longest x1 79.9 us: shard_body(): s_new_row = lax.all_gather(new_s, BOTH, axis=1, tiled=True)]
    pallas_call x0 -> x3, Pallas kernels: none -> 295 us  [the longest x1 158 us: scatter_call(): pl.pallas_call(functools.partial(scatter_kernel, rows), out_shape=jax.Sha...]
    all_gather x1, waiting for transfers between devices: 0.87 us -> 14.9 us  [shard_body(): lax.all_gather(share[:D_ROWS], 'data', axis_index_groups=pair, tiled=True)]
    slice x3 -> x5, local copies, waits for them, and re-layouts: 10.8 us -> 19 us  [the longest x3 15.2 us: shard_body(): a_new_col, s_new_row = (fact_all[:2], fact_all[2:])]
  transfers between devices with their start and end apart: 8 -> 2, of which waited for: 8 -> 2; matrix products, arithmetic and copies ran while one was open for 6% -> 3% of each run, Pallas kernels for 0% -> 0%
where the time goes in v2:
time: 502 us; the launch traced here: 493 us
  Pallas kernels  322 us (64%)
  local copies, waits for them, and re-layouts  56 us (11%)
  waiting for transfers between devices  52.4 us (10%)
  matrix products  42.3 us (8%)
  between operations  16.3 us (3%)
    pallas_call x1, Pallas kernels, scatter_call(): pl.pallas_call(functools.partial(scatter_kernel, rows), out_shape=jax.Sha...  158 us
    pallas_call x2, Pallas kernels, gather_call(): pl.pallas_call(functools.partial(gather_kernel, 0 if plane is None else 1...  137 us
    reduce_scatter x1, waiting for transfers between devices, shard_body(): lax.psum_scatter(jnp.swapaxes(ends, 0, 1), 'data', scatter_dimension=0, t...  37.5 us
    pallas_call x1, Pallas kernels, gram_call(): pl.pallas_call(gram_kernel, out_shape=jax.ShapeDtypeStruct((32, SHARE_ROW...  26.7 us
    slice x3, local copies, waits for them, and re-layouts, shard_body(): a_new_col, s_new_row = (fact_all[:2], fact_all[2:])  15.2 us
    all_gather x1, waiting for transfers between devices, shard_body(): lax.all_gather(share[:D_ROWS], 'data', axis_index_groups=pair, tiled=True)  14.9 us
    dot_general x3, matrix products, matmul(): return jnp.dot(left_mat, right_mat, preferred_element_type=jnp.float32)  14.4 us
    dot_general x3, matrix products, matmul_nt(): lax.dot_general(left_mat, right_mat, NT_DIMS, preferred_element_type=jnp....  14 us
  transfers between devices with their start and end apart: 2, of which 2 were waited for; matrix products, arithmetic and copies ran while one was open for 3% of the time, Pallas kernels for 0%

profile of v2, /device:TPU:0, one launch (start us, length us, event | category | flops | bytes accessed | tf_op | source)
XLA Modules:
  0.0 493.1 jit_solution(3994185877930797195)
XLA Ops:
  10.3 42.7 %weights.1 = bf16[4,2,2,2,512,256]{5,4,3,2,1,0:T(8,128)(2,1)S(1)} custom-call(bf16[512,256]{1,0:T(8,128)(2,1)S(1)} %pad_maximum_fusion.2.refs_0_), custom_call_target="tpu_custom_call" | custom-call | flops 49999998976 | bytes 8388608 | tf_op jit(solution)/shard_map/weights/pallas_call | solution.py:307
  53.1 2.8 fusion.67
  55.9 3.9 copy.59
  59.8 3.6 copy.48
  63.3 1.8 copy.68
  65.2 3.9 copy.60
  69.1 2.0 copy.45
  71.6 1.9 constant_dynamic-slice_fusion.3.x_ref
  73.5 1.8 constant_dynamic-slice_fusion.2.dy_ref
  75.3 4.4 fusion.18
  79.8 4.9 fusion.12
  84.7 5.1 %fusion.11 = (bf16[1024,1024]{1,0:T(8,128)(2,1)}, bf16[1024,1024]{1,0:T(8,128)(2,1)S(1)}) fusion(bf16[1024,1024]{0,1:T(8,128)(2,1)S(1)} %bitcast.133, bf16[1024,1024]{1,0:T(8,128)(2,1)S(1)} %get-tuple-element.41), kind=kOutput, calls=%fused_computation.32 | convolution fusion | flops 2169503744 | bytes 8388608 | tf_op jit(solution)/shard_map/dot_general | solution.py:39
  89.8 4.7 fusion.10.g3_ref
  94.5 4.6 fusion.17.g2_ref
  99.1 4.7 fusion.23.g1_ref
  103.8 26.7 %gram.1 = f32[32,896,256]{2,1,0:T(8,128)} custom-call(bf16[1024,1024]{1,0:T(8,128)(2,1)S(1)} %constant_dynamic-slice_fusion.3.x_ref, bf16[1024,1024]{1,0:T(8,128)(2,1)S(1)} %fusion.23.g1_ref, bf16[1024,1024]{1,0:T(8,128)(2,1)} %copy-done.11, bf16[1024,1024]{1,0:T(8,128)(2,1)} %get-tuple-element.38.h1_ref, bf16[1024,1024]{1,0:T(8,128)(2,1)} %get-tuple-element.40.h2_ref, ...), custom_call_target="tpu_custom_call" | custom-call | flops 15000000512 | bytes 46000000 | tf_op jit(solution)/shard_map/gram/pallas_call | solution.py:122
  130.5 158.4 %sums.1 = f32[896,256]{1,0:T(8,128)} custom-call(f32[4,2,2,2,896,256]{5,4,3,2,1,0:T(8,128)} %bitcast.149), custom_call_target="tpu_custom_call" | custom-call | flops 120000004096 | bytes 60000000 | tf_op jit(solution)/shard_map/sums/pallas_call | solution.py:473
  288.9 1.9 slice.100
  290.9 6.5 %fusion.40 = f32[256,1024]{1,0:T(8,128)S(1)} fusion(bf16[4096,1024]{1,0:T(8,128)(2,1)} %param.12, s32[]{:T(128)S(6)} %select_n.61), kind=kOutput, calls=%fused_computation.64 | convolution fusion | flops 2147483648 | bytes 11534340 | tf_op jit(solution)/shard_map/dot_general | solution.py:43
  297.5 2.4 fusion.38
  299.8 1.6 maximum_bitcast_fusion
  302.6 14.9 %all-gather.2.cloned.1.call-done = f32[1024,256]{1,0:T(8,128)} async-done(((f32[512,256]{1,0:T(8,128)}), f32[1024,256]{1,0:T(8,128)}) %all-gather.2.cloned.1.call-update) | async-done | bytes 1048592 | tf_op jit(solution)/shard_map/all_gather | solution.py:535
  317.5 4.3 fusion.33
  322.5 37.5 %reduce-scatter.2.cloned.1.call-done = f32[1,2,32,1024]{3,2,1,0:T(8,128)} async-done(((f32[8,2,32,1024]{3,2,1,0:T(8,128)}), f32[1,2,32,1024]{3,2,1,0:T(8,128)}) %reduce-scatter.2.cloned.1.call-update) | async-done | bytes 262160 | tf_op jit(solution)/shard_map/reduce_scatter | solution.py:512
  362.2 94.3 %results.1 = (f32[4,2,2,2,128,1024]{5,4,3,2,1,0:T(8,128)S(1)}, f32[2,2,2,640,256]{4,3,2,1,0:T(8,128)S(1)}) custom-call(f32[128,1024]{1,0:T(8,128)S(1)} %bitcast.119, f32[640,256]{1,0:T(8,128)S(1)} %pad_maximum_fusion.refs_1_), custom_call_target="tpu_custom_call" | custom-call | flops 49999998976 | bytes 22020096 | tf_op jit(solution)/shard_map/results/pallas_call | solution.py:307
  456.5 5.7 %copy-done.2 = f32[4,2,2,2,128,1024]{5,4,3,2,1,0:T(8,128)} copy-done((f32[4,2,2,2,128,1024]{5,4,3,2,1,0:T(8,128)}, f32[4,2,2,2,128,1024]{5,4,3,2,1,0:T(8,128)S(1)}, u32[]{:S(2)}) %copy-start.2) | copy-done | bytes 16777240
  463.6 6.7 %fusion.66 = (f32[2,32,32,1024]{3,2,0,1:T(8,128)S(1)}, f32[2,32,32,1024]{3,2,0,1:T(8,128)S(1)}) fusion(f32[4,32,32,1024]{3,2,0,1:T(8,128)} %bitcast.115), kind=kLoop, calls=%fused_computation.106 | loop fusion | bytes 33554432 | tf_op jit(solution)/shard_map/slice | solution.py:554
  470.3 4.2 copy.54
  474.5 4.2 copy.57
  478.8 1.6 slice_bitcast_fusion
  480.4 1.8 copy.58
  482.2 1.3 fusion.68
  (50 shorter events, 9.8 us)
Async XLA Ops:
  8.0 1.2 copy-start
  8.0 309.5 %all-gather.2.cloned.1.call-start = ((), (), s32[]{:S(2)}) async-start(), calls=%async_computation.2 | async-start | bytes 1572864 | tf_op jit(solution)/shard_map/all_gather | solution.py:535
  71.6 3.7 copy-start.3
  75.3 14.5 %copy-start.6 = (bf16[1024,1024]{1,0:T(8,128)(2,1)}, bf16[1024,1024]{1,0:T(8,128)(2,1)S(1)}, u32[]{:S(2)}) copy-start(bf16[1024,1024]{1,0:T(8,128)(2,1)S(1)} %constant_dynamic-slice_fusion.2.dy_ref) | copy-start | bytes 6291460
  75.3 4.5 copy-start.4
  79.7 4.9 copy-start.5
  94.4 4.7 copy-start.10
  99.1 4.7 copy-start.11
  290.8 69.2 %reduce-scatter.2.cloned.1.call-start = ((), (), s32[]{:S(2)}) async-start(), calls=%async_computation.1 | async-start | bytes 2359296 | tf_op jit(solution)/shard_map/reduce_scatter | solution.py:512
  290.9 6.6 %copy-start.7 = (bf16[4096,1024]{1,0:T(8,128)(2,1)S(1)}, bf16[4096,1024]{1,0:T(8,128)(2,1)}, u32[]{:S(2)}) copy-start(bf16[4096,1024]{1,0:T(8,128)(2,1)} %param.13) | copy-start | bytes 25165828
  299.8 1.7 slice-start.1
  299.8 1.8 slice-start
  301.4 20.4 %copy-start.8 = (f32[2,256,256]{2,1,0:T(8,128)S(1)}, f32[2,256,256]{2,1,0:T(8,128)}, u32[]{:S(2)}) copy-start(f32[2,256,256]{2,1,0:T(8,128)} %param.22) | copy-start | bytes 1572868
  301.5 20.4 %copy-start.9 = (f32[2,256,256]{2,1,0:T(8,128)S(1)}, f32[2,256,256]{2,1,0:T(8,128)}, u32[]{:S(2)}) copy-start(f32[2,256,256]{2,1,0:T(8,128)} %param.21) | copy-start | bytes 1572868
  456.5 5.7 %copy-start.2 = (f32[4,2,2,2,128,1024]{5,4,3,2,1,0:T(8,128)}, f32[4,2,2,2,128,1024]{5,4,3,2,1,0:T(8,128)S(1)}, u32[]{:S(2)}) copy-start(f32[4,2,2,2,128,1024]{5,4,3,2,1,0:T(8,128)S(1)} %get-tuple-element.9) | copy-start | bytes 50331652
  480.4 4.8 copy-start.1
Sparse Core Ops, SparseCore 0:
  291.0 26.5 all-gather.1
Sparse Core Ops, SparseCore 1:
  301.5 58.4 reduce-scatter.1

commit v3 on v2

v3 whole, which is shorter than its diff:
```python
import functools
import math
import jax
import jax.numpy as jnp
from jax import lax
from jax.sharding import PartitionSpec as P
from jax.experimental import pallas as pl
from jax.experimental.pallas import tpu as pltpu

FACTOR_DECAY = 0.8
GELU_SCALE = math.sqrt(2.0 / math.pi)
GELU_CUBIC = 0.044715
EXACT = lax.Precision.HIGHEST
TN_DIMS = (((0,), (0,)), ((), ()))
NT_DIMS = (((1,), (1,)), ((), ()))
BOTH = ('model', 'data')


def gelu_value(pre_act):
    tanh_arg = GELU_SCALE * (pre_act + GELU_CUBIC * pre_act * pre_act * pre_act)
    return 0.5 * pre_act * (1.0 + jnp.tanh(tanh_arg))


def gelu_slope(pre_act):
    tanh_arg = GELU_SCALE * (pre_act + GELU_CUBIC * pre_act * pre_act * pre_act)
    tanh_val = jnp.tanh(tanh_arg)
    return 0.5 * (1.0 + tanh_val) + 0.5 * pre_act * (1.0 - tanh_val * tanh_val) * GELU_SCALE * (1.0 + 3.0 * GELU_CUBIC * pre_act * pre_act)


def activate(pre_act):
    return gelu_value(pre_act.astype(jnp.float32)).astype(jnp.bfloat16)


def back_gate(grad_act, pre_act):
    return (grad_act.astype(jnp.float32) * gelu_slope(pre_act.astype(jnp.float32))).astype(jnp.bfloat16)


def matmul(left_mat, right_mat):
    return jnp.dot(left_mat, right_mat, preferred_element_type=jnp.float32)


def matmul_tn(left_mat, right_mat):
    return lax.dot_general(left_mat, right_mat, TN_DIMS, preferred_element_type=jnp.float32)


def matmul_nt(left_mat, right_mat):
    return lax.dot_general(left_mat, right_mat, NT_DIMS, preferred_element_type=jnp.float32)


def exact_dot(left_mat, right_mat):
    return jnp.dot(left_mat, right_mat, precision=EXACT, preferred_element_type=jnp.float32)


MIB = 1024 * 1024
BLOCK = 256
HIDDEN = 1024
D_ROWS = 512
FULL_BASE = 512
BLOCK_BASE = 768
SHARE_ROWS = 896


def gram_kernel(x_ref, g1_ref, g2_ref, h1_ref, h2_ref, g3_ref, dy_ref, h3_ref, out_ref,
                act, stage, bstage, in_sem, out_sem, b_sem):
    sources = [dy_ref, h3_ref, h2_ref, g3_ref, g2_ref, h1_ref, x_ref, g1_ref]
    slots = [3, 7, 2, 6, 1, 5, 0, 4]
    loads = [pltpu.make_async_copy(src, act.at[slot], in_sem.at[slot]) for src, slot in zip(sources, slots)]
    for load in loads:
        load.start()
    started = [0]
    pend = {}

    def out_copy(slot, dst):
        return pltpu.make_async_copy(stage.at[slot], dst, out_sem.at[slot])

    for layer in (3, 2, 1, 0):
        pltpu.make_async_copy(x_ref, act.at[layer], in_sem.at[layer]).wait()
        pltpu.make_async_copy(x_ref, act.at[4 + layer], in_sem.at[4 + layer]).wait()

        def d_body(m, carry, layer=layer):
            slot = lax.rem(m, 2)
            cols = pl.ds(pl.multiple_of(m * BLOCK, BLOCK), BLOCK)
            right = act[4 + layer, :, cols]
            dst = out_ref.at[pl.ds(m * 8 + 2 * layer, 2), pl.ds(0, D_ROWS)]

            if layer == 3:
                @pl.when(m >= 2)
                def _():
                    out_copy(slot, dst).wait()
                    pltpu.make_async_copy(bstage.at[slot], out_ref.at[pl.ds(0, 8), pl.ds(BLOCK_BASE, 32)], b_sem.at[slot]).wait()
            else:
                out_copy(slot, dst).wait()
                pltpu.make_async_copy(bstage.at[slot], out_ref.at[pl.ds(0, 8), pl.ds(BLOCK_BASE, 32)], b_sem.at[slot]).wait()
            prod = lax.dot_general(act[layer], right, TN_DIMS, preferred_element_type=jnp.float32)
            stage[slot] = prod.reshape(2, D_ROWS, BLOCK)
            out_copy(slot, dst).start()
            blk = lax.dot_general(right, right, TN_DIMS, preferred_element_type=jnp.float32)
            bstage[slot] = blk.reshape(8, 32, BLOCK)
            pltpu.make_async_copy(bstage.at[slot], out_ref.at[pl.ds(m * 8, 8), pl.ds(BLOCK_BASE + 32 * layer, 32)], b_sem.at[slot]).start()
            return carry

        lax.fori_loop(0, 4, d_body, 0)

        if layer in (2, 1):
            which = 0 if layer == 2 else 1

            def f_body(n, carry, layer=layer, which=which):
                slot = lax.rem(n, 2)
                cols = pl.ds(pl.multiple_of(n * BLOCK, BLOCK), BLOCK)
                dst = out_ref.at[pl.ds(n * 8, 8), pl.ds(FULL_BASE + which * 128, 128)]
                pltpu.make_async_copy(stage.at[slot], out_ref.at[pl.ds(0, 2), pl.ds(0, D_ROWS)], out_sem.at[slot]).wait()
                prod = lax.dot_general(act[layer], act[layer, :, cols], TN_DIMS, preferred_element_type=jnp.float32)
                stage[slot] = prod.reshape(2, D_ROWS, BLOCK)
                pltpu.make_async_copy(stage.at[slot].reshape(8, 128, BLOCK), dst, out_sem.at[slot]).start()
                return carry

            lax.fori_loop(0, 4, f_body, 0)
    for slot in range(2):
        pltpu.make_async_copy(stage.at[slot], out_ref.at[pl.ds(0, 2), pl.ds(0, D_ROWS)], out_sem.at[slot]).wait()
        pltpu.make_async_copy(bstage.at[slot], out_ref.at[pl.ds(0, 8), pl.ds(BLOCK_BASE, 32)], b_sem.at[slot]).wait()


def gram_call(x_loc, g_one, g_two, h_one, h_two, g_three, dy_loc, h_three):
    any_spec = pl.BlockSpec(memory_space=pl.ANY)
    return pl.pallas_call(
        gram_kernel,
        out_shape=jax.ShapeDtypeStruct((32, SHARE_ROWS, BLOCK), jnp.float32),
        in_specs=[any_spec] * 8,
        out_specs=any_spec,
        scratch_shapes=[
            pltpu.VMEM((8, HIDDEN, HIDDEN), jnp.bfloat16),
            pltpu.VMEM((2, 2, D_ROWS, BLOCK), jnp.float32),
            pltpu.VMEM((2, 8, 32, BLOCK), jnp.float32),
            pltpu.SemaphoreType.DMA((8,)),
            pltpu.SemaphoreType.DMA((2,)),
            pltpu.SemaphoreType.DMA((2,)),
        ],
        compiler_params=pltpu.CompilerParams(vmem_limit_bytes=48 * HIDDEN * HIDDEN),
        cost_estimate=pl.CostEstimate(flops=15_000_000_000, bytes_accessed=46_000_000, transcendentals=0),
        name='gram',
    )(x_loc, g_one, g_two, h_one, h_two, g_three, dy_loc, h_three)


MESH_ID = pl.DeviceIdType.MESH
CHUNK_ORDER = ((0, 0), (3, 0), (0, 1), (3, 1), (1, 0), (2, 0), (1, 1), (2, 1))


def torus_place():
    z = lax.axis_index('model')
    d = lax.axis_index('data')
    y = d // 4
    x = (d // 2) % 2
    c = d % 2
    near = {'x': (z, d + 2 - 4 * x), 'y': (z, d + 4 - 8 * y), 'c': (z, d + 1 - 2 * c), 'up': (z + 1, d), 'dn': (z - 1, d)}
    return z, y, x, c, near


def meet_neighbours(z, near):
    barrier = pltpu.get_barrier_semaphore()
    for side in ('x', 'y', 'c'):
        pl.semaphore_signal(barrier, inc=1, device_id=near[side], device_id_type=MESH_ID)

    @pl.when(z < 3)
    def _():
        pl.semaphore_signal(barrier, inc=1, device_id=near['up'], device_id_type=MESH_ID)

    @pl.when(z > 0)
    def _():
        pl.semaphore_signal(barrier, inc=1, device_id=near['dn'], device_id_type=MESH_ID)
    pl.semaphore_wait(barrier, 3 + (z + 3) // 4 + (6 - z) // 4)


def remote(src, dst, send_sem, recv_sem, where):
    return pltpu.make_async_remote_copy(src_ref=src, dst_ref=dst, send_sem=send_sem, recv_sem=recv_sem, device_id=where, device_id_type=MESH_ID)


def gather_kernel(plan, *refs):
    n = len(plan.items)
    pieces, outs, lands = refs[:plan.n_in], refs[plan.n_in:plan.n_in + n], refs[plan.n_in + n:plan.n_in + 2 * n]
    load_sem, z_recv, x_recv, y_recv, d_recv, c_recv, up_send, dn_send, x_send, y_send, dy_send, dx_send, c_send, flush_sem = refs[plan.n_in + 2 * n:]
    z, y, x, c, near = torus_place()

    def slot(ref, j, zs, yy, xx, cc):
        return plan.items[j].slot(ref, zs, 4 * yy + 2 * xx + cc)

    def view(j, zs, yy, xx, cc):
        return slot(lands[j], j, zs, yy, xx, cc)

    def half(j, zs, yy, xx, cc, which):
        return plan.items[j].half(lands[j], zs, 4 * yy + 2 * xx + cc, which)

    def flush(j, zs, yy, xx, cc, index):
        return pltpu.make_async_copy(view(j, zs, yy, xx, cc), slot(outs[j], j, zs, yy, xx, cc), flush_sem.at[j, zs, index])

    loads = [pltpu.make_async_copy(item.piece(pieces, z, 4 * y + 2 * x + c), view(j, z, y, x, c), load_sem.at[j]) for j, item in enumerate(plan.items)]
    for load in loads:
        load.start()
    meet_neighbours(z, near)

    def side_copy(j, zs, side):
        send, recv = {'x': (x_send, x_recv), 'y': (y_send, y_recv), 'up': (up_send, z_recv), 'dn': (dn_send, z_recv)}[side]
        return remote(view(j, zs, y, x, c), view(j, zs, y, x, c), send.at[j, zs], recv.at[j, zs], near[side])

    def from_side(j, zs, side):
        yy, xx = (y, 1 - x) if side == 'x' else (1 - y, x)
        send, recv = {'x': (x_send, x_recv), 'y': (y_send, y_recv)}[side]
        return remote(view(j, zs, yy, xx, c), view(j, zs, yy, xx, c), send.at[j, zs], recv.at[j, zs], near[side])

    def dy_copy(j, zs):
        return remote(half(j, zs, y, 1 - x, c, 0), half(j, zs, y, 1 - x, c, 0), dy_send.at[j, zs], d_recv.at[j, zs, 0], near['y'])

    def dx_copy(j, zs):
        return remote(half(j, zs, 1 - y, x, c, 1), half(j, zs, 1 - y, x, c, 1), dx_send.at[j, zs], d_recv.at[j, zs, 1], near['x'])

    def kind_place(kind):
        return (y if kind < 2 else 1 - y), (x if kind % 2 == 0 else 1 - x)

    def c_copy(j, zs, kind):
        yy, xx = kind_place(kind)
        return remote(view(j, zs, yy, xx, c), view(j, zs, yy, xx, c), c_send.at[j, zs, kind], c_recv.at[j, zs, kind], near['c'])

    def share_core(j, zs, kind):
        yy, xx = kind_place(kind)
        c_copy(j, zs, kind).start()
        flush(j, zs, yy, xx, c, kind).start()

    def guard(off, body):
        if off == 0:
            body(z)
        elif off < 0:
            pl.when(z >= -off)(lambda: body(z + off))
        else:
            pl.when(z <= 3 - off)(lambda: body(z + off))

    def z_step(j, off):
        def body(zs):
            if off == 0:
                loads[j].wait()
            else:
                side_copy(j, zs, 'up').wait_recv()
            if off <= 0 and not plan.items[j].plane:
                pl.when(z < 3)(lambda: side_copy(j, zs, 'up').start())
            if off >= 0 and not plan.items[j].plane:
                pl.when(z > 0)(lambda: side_copy(j, zs, 'dn').start())
            side_copy(j, zs, 'x').start()
            side_copy(j, zs, 'y').start()
            share_core(j, zs, 0)
        guard(off, body)

    def xy_step(j, off):
        def body(zs):
            from_side(j, zs, 'x').wait_recv()
            dy_copy(j, zs).start()
            share_core(j, zs, 1)
            from_side(j, zs, 'y').wait_recv()
            dx_copy(j, zs).start()
            share_core(j, zs, 2)
        guard(off, body)

    def diag_step(j, off):
        def body(zs):
            for which in range(2):
                remote(half(j, zs, 1 - y, 1 - x, c, which), half(j, zs, 1 - y, 1 - x, c, which), dy_send.at[j, zs], d_recv.at[j, zs, which], near['y']).wait_recv()
            share_core(j, zs, 3)
        guard(off, body)

    def core_step(j, off):
        def body(zs):
            for kind in range(4):
                yy, xx = kind_place(kind)
                remote(view(j, zs, yy, xx, 1 - c), view(j, zs, yy, xx, 1 - c), c_send.at[j, zs, kind], c_recv.at[j, zs, kind], near['c']).wait_recv()
                flush(j, zs, yy, xx, 1 - c, 4 + kind).start()
        guard(off, body)

    def last_step(j, off):
        def body(zs):
            for kind in range(4):
                yy, xx = kind_place(kind)
                c_copy(j, zs, kind).wait_send()
                flush(j, zs, yy, xx, c, kind).wait()
                flush(j, zs, yy, xx, 1 - c, 4 + kind).wait()
            side_copy(j, zs, 'x').wait_send()
            side_copy(j, zs, 'y').wait_send()
            dy_copy(j, zs).wait_send()
            dx_copy(j, zs).wait_send()
            if off <= 0 and not plan.items[j].plane:
                pl.when(z < 3)(lambda: side_copy(j, zs, 'up').wait_send())
            if off >= 0 and not plan.items[j].plane:
                pl.when(z > 0)(lambda: side_copy(j, zs, 'dn').wait_send())
        guard(off, body)

    waves = [[(j, 0) for j in plan.order]]
    for far in range(1, 4):
        waves.append([(j, sign * far) for j in plan.order if not plan.items[j].plane for sign in (-1, 1)])
    for step in range(7):
        for func, lag in ((z_step, 0), (xy_step, 1), (diag_step, 2), (core_step, 3)):
            if 0 <= step - lag < 4:
                for j, off in waves[step - lag]:
                    func(j, off)
    for wave in waves:
        for j, off in wave:
            last_step(j, off)


class Item:
    def __init__(self, shape, dtype, piece, slot, half, plane=False):
        self.shape, self.dtype, self.piece, self.slot, self.half, self.plane = shape, dtype, piece, slot, half, plane


class Plan:
    def __init__(self, n_in, items, order):
        self.n_in, self.items, self.order = n_in, items, order


def gather_call(args, items, order, collective_id, name):
    n = len(items)
    dma = pltpu.SemaphoreType.DMA
    size = sum(math.prod(item.shape) * jnp.dtype(item.dtype).itemsize for item in items)
    hbm = pl.BlockSpec(memory_space=pltpu.HBM)
    flat = dma((n, 4))
    return pl.pallas_call(
        functools.partial(gather_kernel, Plan(len(args), items, order)),
        out_shape=[jax.ShapeDtypeStruct(item.shape, item.dtype) for item in items],
        in_specs=[hbm] * len(args),
        out_specs=[hbm] * n,
        scratch_shapes=[pltpu.VMEM(item.shape, item.dtype) for item in items]
        + [dma((n,)), flat, flat, flat, dma((n, 4, 2)), dma((n, 4, 4)), flat, flat, flat, flat, flat, flat, dma((n, 4, 4)), dma((n, 4, 8))],
        compiler_params=pltpu.CompilerParams(collective_id=collective_id, has_side_effects=True, vmem_limit_bytes=size + 8 * MIB),
        cost_estimate=pl.CostEstimate(flops=50_000_000_000, bytes_accessed=size, transcendentals=0),
        name=name,
    )(*args)


def col_slot(ref, zs, d):
    return ref.at[pl.ds(d * 128, 128), pl.ds(zs * BLOCK, BLOCK)]


def col_half(ref, zs, d, which):
    return ref.at[pl.ds(d * 128 + which * 64, 64), pl.ds(zs * BLOCK, BLOCK)]


def row_slot(ref, zs, d):
    return ref.at[pl.ds((zs * 8 + d) * 32, 32)]


def row_half(ref, zs, d, which):
    return ref.at[pl.ds((zs * 8 + d) * 32 + which * 16, 16)]


def gather_weights(w_col, w_row):
    shape = (HIDDEN, HIDDEN)
    items = [Item(shape, w_col.dtype, lambda refs, z, d, i=i: refs[0].at[i, pl.ds(d * 128, 128)], col_slot, col_half) for i in range(2)]
    items += [Item(shape, w_row.dtype, lambda refs, z, d, i=i: refs[1].at[i, pl.ds(d * 32, 32)], row_slot, row_half) for i in range(2)]
    return gather_call((w_col, w_row), items, (0, 3, 2, 1), 1, 'weights')


def gather_results(facts, u_half, blocks):
    items = [
        Item((4, HIDDEN, HIDDEN), facts.dtype, lambda refs, z, d: refs[0],
             lambda ref, zs, d: ref.at[:, pl.ds(d * 128, 128), pl.ds(zs * BLOCK, BLOCK)],
             lambda ref, zs, d, which: ref.at[pl.ds(2 * which, 2), pl.ds(d * 128, 128), pl.ds(zs * BLOCK, BLOCK)]),
        Item((8, D_ROWS, BLOCK), facts.dtype, lambda refs, z, d: refs[1],
             lambda ref, zs, d: ref.at[d], lambda ref, zs, d, which: ref.at[d, pl.ds(which * BLOCK, BLOCK)], True),
        Item((4, BLOCK, BLOCK), facts.dtype, lambda refs, z, d: refs[2],
             lambda ref, zs, d: ref.at[:, pl.ds(d * 32, 32)], lambda ref, zs, d, which: ref.at[pl.ds(2 * which, 2), pl.ds(d * 32, 32)], True),
    ]
    return gather_call((facts, u_half, blocks), items, (1, 2, 0), 3, 'results')


def add_into(dst, src, rows):
    step = 32 if rows % 32 == 0 else 16 if rows % 16 == 0 else 8

    def body(i, carry):
        span = pl.ds(pl.multiple_of(i * step, 8), step)
        dst[span, :] = dst[span, :] + src[span, :]
        return carry

    lax.fori_loop(0, rows // step, body, 0)


def scatter_kernel(rows, parts_ref, ends_ref, share_ref, eshare_ref, grad_ref, own, mate, one_x, one_y, two_x, two_y, up_buf, dn_buf,
                   eown, emate, eone, etwo, gland, e_sem, emate_sem, eone_sem, etwo_sem, g_sem, out2_sem,
                   own_sem, mate_send, mate_recv, x1_send, x1_recv, y1_send, y1_recv, x2_send, x2_recv, y2_send, y2_recv,
                   up_send, up_recv, dn_send, dn_recv, out_sem):
    z, y, x, c, near = torus_place()
    sub = rows // 4
    eload = pltpu.make_async_copy(ends_ref.at[:, :, :, c], eown, e_sem.at[0])
    eload.start()
    loads = {}
    for k, (zd, h) in enumerate(CHUNK_ORDER):
        loads[k] = []
        for col in range(2):
            span = pl.ds(col * 2 * sub + h * sub, sub)
            load = pltpu.make_async_copy(parts_ref.at[zd, :, :, c, span], own.at[zd, :, :, span], own_sem.at[k, col])
            load.start()
            loads[k].append(load)
    meet_neighbours(z, near)
    ematec = remote(ends_ref.at[:, :, :, 1 - c], emate, emate_sem.at[0], emate_sem.at[1], near['c'])
    ematec.start()
    eones = (remote(eown.at[0, :, 1 - x], eone.at[0], eone_sem.at[0], eone_sem.at[1], near['x']),
             remote(eown.at[1, 1 - y], eone.at[1], eone_sem.at[2], eone_sem.at[3], near['y']))
    etwos = (remote(eown.at[0, 1 - y, x], etwo.at[0], etwo_sem.at[0], etwo_sem.at[1], near['y']),
             remote(eown.at[1, y, 1 - x], etwo.at[1], etwo_sem.at[2], etwo_sem.at[3], near['x']))
    mates = {}
    for k, (zd, h) in enumerate(CHUNK_ORDER):
        mates[k] = []
        for col in range(2):
            span = pl.ds(col * 2 * sub + h * sub, sub)
            copy = remote(parts_ref.at[zd, :, :, 1 - c, span], mate.at[zd, :, :, span], mate_send.at[k, col], mate_recv.at[k, col], near['c'])
            copy.start()
            mates[k].append(copy)

    def spans(h):
        return pl.ds(h * sub, sub), pl.ds(2 * sub + h * sub, sub)

    def one_copies(k):
        zd, h = CHUNK_ORDER[k]
        first, second = spans(h)
        piece = pl.ds(h * sub, sub)
        return (remote(own.at[zd, :, 1 - x, first], one_x.at[zd, :, piece], x1_send.at[k], x1_recv.at[k], near['x']),
                remote(own.at[zd, 1 - y, :, second], one_y.at[zd, :, piece], y1_send.at[k], y1_recv.at[k], near['y']))

    def two_copies(k):
        zd, h = CHUNK_ORDER[k]
        first, second = spans(h)
        piece = pl.ds(h * sub, sub)
        return (remote(own.at[zd, 1 - y, x, first], two_y.at[zd, piece], y2_send.at[k], y2_recv.at[k], near['y']),
                remote(own.at[zd, y, 1 - x, second], two_x.at[zd, piece], x2_send.at[k], x2_recv.at[k], near['x']))

    def z_copies(k):
        zd, h = CHUNK_ORDER[k]
        out = []
        for col, span in enumerate(spans(h)):
            out.append((remote(own.at[zd, y, x, span], up_buf.at[zd, span], dn_send.at[k, col], up_recv.at[k, col], near['dn']),
                        remote(own.at[zd, y, x, span], dn_buf.at[zd, span], up_send.at[k, col], dn_recv.at[k, col], near['up'])))
        return out

    def step_a(k):
        zd, h = CHUNK_ORDER[k]
        first, second = spans(h)
        ones = one_copies(k)
        loads[k][0].wait()
        mates[k][0].wait_recv()
        for yy in range(2):
            add_into(own.at[zd, yy, 1 - x, first], mate.at[zd, yy, 1 - x, first], sub)
        ones[0].start()
        loads[k][1].wait()
        mates[k][1].wait_recv()
        for xx in range(2):
            add_into(own.at[zd, 1 - y, xx, second], mate.at[zd, 1 - y, xx, second], sub)
        ones[1].start()
        for yy in range(2):
            add_into(own.at[zd, yy, x, first], mate.at[zd, yy, x, first], sub)
        for xx in range(2):
            add_into(own.at[zd, y, xx, second], mate.at[zd, y, xx, second], sub)

    def step_b(k):
        zd, h = CHUNK_ORDER[k]
        first, second = spans(h)
        piece = pl.ds(h * sub, sub)
        ones, twos = one_copies(k), two_copies(k)
        ones[0].wait_recv()
        add_into(own.at[zd, 1 - y, x, first], one_x.at[zd, 1 - y, piece], sub)
        twos[0].start()
        ones[1].wait_recv()
        add_into(own.at[zd, y, 1 - x, second], one_y.at[zd, 1 - x, piece], sub)
        twos[1].start()
        add_into(own.at[zd, y, x, first], one_x.at[zd, y, piece], sub)
        add_into(own.at[zd, y, x, second], one_y.at[zd, x, piece], sub)

    def step_c(k):
        zd, h = CHUNK_ORDER[k]
        first, second = spans(h)
        piece = pl.ds(h * sub, sub)
        twos = two_copies(k)
        zcs = z_copies(k)
        for col, (copy, buf, span) in enumerate(((twos[0], two_y, first), (twos[1], two_x, second))):
            copy.wait_recv()
            add_into(own.at[zd, y, x, span], buf.at[zd, piece], sub)

            @pl.when((z < 3) & (z >= zd))
            def _(col=col, span=span):
                zcs[col][0].wait_recv()
                add_into(own.at[zd, y, x, span], up_buf.at[zd, span], sub)

            @pl.when((z > 0) & (z <= zd))
            def _(col=col, span=span):
                zcs[col][1].wait_recv()
                add_into(own.at[zd, y, x, span], dn_buf.at[zd, span], sub)
            pl.when(z > zd)(lambda: zcs[col][0].start())
            pl.when(z < zd)(lambda: zcs[col][1].start())

            @pl.when(z == zd)
            def _(col=col, span=span):
                pltpu.make_async_copy(own.at[zd, y, x, span], share_ref.at[span], out_sem.at[h, col]).start()

    def ends_a():
        eload.wait()
        ematec.wait_recv()
        for mat in range(2):
            for yy in range(2):
                for xx in range(2):
                    add_into(eown.at[mat, yy, xx], emate.at[mat, yy, xx], 128)
            eones[mat].start()

    def ends_b():
        eones[0].wait_recv()
        for yy in range(2):
            add_into(eown.at[0, yy, x], eone.at[0, yy], 128)
        etwos[0].start()
        eones[1].wait_recv()
        for xx in range(2):
            add_into(eown.at[1, y, xx], eone.at[1, xx], 128)
        etwos[1].start()

    def ends_c():
        for mat in range(2):
            etwos[mat].wait_recv()
            add_into(eown.at[mat, y, x], etwo.at[mat], 128)
            pltpu.make_async_copy(eown.at[mat, y, x], eshare_ref.at[mat], out2_sem.at[mat]).start()

    n = len(CHUNK_ORDER)
    ends_a()
    for step in range(n + 3):
        if step == 1:
            ends_b()
        if step == 2:
            ends_c()
        if step < n:
            step_a(step)
        if 0 <= step - 1 < n:
            step_b(step - 1)
        if 0 <= step - 3 < n:
            step_c(step - 3)
    mine = own.at[z, y, x, pl.ds(0, D_ROWS)]
    gcopy = remote(mine, gland, g_sem.at[0], g_sem.at[1], near['c'])
    gcopy.start()
    gout = pltpu.make_async_copy(mine, grad_ref.at[c], out2_sem.at[2])
    gout.start()
    gcopy.wait_recv()
    gmate = pltpu.make_async_copy(gland, grad_ref.at[1 - c], out2_sem.at[3])
    gmate.start()
    for copy in (ematec, gcopy) + eones + etwos:
        copy.wait_send()
    for k, (zd, h) in enumerate(CHUNK_ORDER):
        for copy in mates[k] + list(one_copies(k)) + list(two_copies(k)):
            copy.wait_send()
        for col, (down, up) in enumerate(z_copies(k)):
            pl.when(z > zd)(lambda: down.wait_send())
            pl.when(z < zd)(lambda: up.wait_send())
    for h in range(2):
        for col in range(2):
            span = spans(h)[col]
            pltpu.make_async_copy(own.at[0, y, x, span], share_ref.at[span], out_sem.at[h, col]).wait()
    for mat in range(2):
        pltpu.make_async_copy(eown.at[mat, y, x], eshare_ref.at[mat], out2_sem.at[mat]).wait()
    gout.wait()
    gmate.wait()


def scatter_call(parts, ends, collective_id, name):
    rows = parts.shape[-2]
    half = rows // 2
    f32 = jnp.float32
    dma = pltpu.SemaphoreType.DMA
    n = len(CHUNK_ORDER)
    whole = pltpu.VMEM((4, 2, 2, rows, BLOCK), f32)
    one_buf = pltpu.VMEM((4, 2, half, BLOCK), f32)
    two_buf = pltpu.VMEM((4, half, BLOCK), f32)
    z_buf = pltpu.VMEM((4, rows, BLOCK), f32)
    e_buf = pltpu.VMEM((2, 2, 2, 128, BLOCK), f32)
    hbm = pl.BlockSpec(memory_space=pltpu.HBM)
    return pl.pallas_call(
        functools.partial(scatter_kernel, rows),
        out_shape=[jax.ShapeDtypeStruct((rows, BLOCK), f32), jax.ShapeDtypeStruct((2, 128, BLOCK), f32), jax.ShapeDtypeStruct((2, D_ROWS, BLOCK), f32)],
        in_specs=[hbm] * 2,
        out_specs=[hbm] * 3,
        scratch_shapes=[whole, whole, one_buf, one_buf, two_buf, two_buf, z_buf, z_buf,
                        e_buf, e_buf, pltpu.VMEM((2, 2, 128, BLOCK), f32), pltpu.VMEM((2, 128, BLOCK), f32), pltpu.VMEM((D_ROWS, BLOCK), f32),
                        dma((1,)), dma((2,)), dma((4,)), dma((4,)), dma((2,)), dma((4,))]
        + [dma((n, 2))] * 3 + [dma((n,))] * 8 + [dma((n, 2))] * 4 + [dma((2, 2))],
        compiler_params=pltpu.CompilerParams(collective_id=collective_id, has_side_effects=True, vmem_limit_bytes=60 * MIB),
        cost_estimate=pl.CostEstimate(flops=120_000_000_000, bytes_accessed=60 * MIB, transcendentals=0),
        name=name,
    )(parts.reshape(4, 2, 2, 2, rows, BLOCK), ends.reshape(2, 2, 2, 2, 128, BLOCK))


def solution(mesh):
    data_ways = mesh.shape['data']
    model_ways = mesh.shape['model']

    def shard_body(x_tokens, dy_tokens, w_col, w_row, a_old_col, s_old_col, a_old_row, s_old_row, a_inv_col, s_inv_col, a_inv_row, s_inv_row):
        model_id = lax.axis_index('model')
        data_id = lax.axis_index('data')
        inv_rows = 1.0 / (x_tokens.shape[0] * data_ways)
        w_one, w_three, w_two, w_four = gather_weights(w_col, w_row)
        x_cols = lax.dynamic_slice(x_tokens, (0, BLOCK * model_id), (x_tokens.shape[0], BLOCK))
        dy_cols = lax.dynamic_slice(dy_tokens, (0, BLOCK * model_id), (x_tokens.shape[0], BLOCK))
        ends = jnp.stack([matmul_tn(x_tokens, x_cols), matmul_tn(dy_tokens, dy_cols)])
        rows_dev = x_tokens.shape[0] // model_ways
        x_loc = lax.dynamic_slice(x_tokens, (rows_dev * model_id, 0), (rows_dev, HIDDEN))
        dy_loc = lax.dynamic_slice(dy_tokens, (rows_dev * model_id, 0), (rows_dev, HIDDEN))
        z_one = matmul(x_loc, w_one).astype(jnp.bfloat16)
        h_one = activate(z_one)
        z_two = matmul(h_one, w_two).astype(jnp.bfloat16)
        h_two = activate(z_two)
        z_three = matmul(h_two, w_three).astype(jnp.bfloat16)
        h_three = activate(z_three)
        g_three = back_gate(matmul_nt(dy_loc, w_four).astype(jnp.bfloat16), z_three)
        g_two = back_gate(matmul_nt(g_three, w_three).astype(jnp.bfloat16), z_two)
        g_one = back_gate(matmul_nt(g_two, w_two).astype(jnp.bfloat16), z_one)
        parts = gram_call(x_loc, g_one, g_two, h_one, h_two, g_three, dy_loc, h_three)
        share, eshare, grad_mat = scatter_call(parts, ends, 2, 'sums')
        keep = 1.0 - FACTOR_DECAY
        spot = (0, 128 * data_id, BLOCK * model_id)
        mids = share[FULL_BASE:BLOCK_BASE].reshape(2, 128, BLOCK)
        sums = jnp.stack([eshare[0], mids[0], mids[1], eshare[1]])
        olds = jnp.concatenate([lax.dynamic_slice(old, spot, (2, 128, BLOCK)) for old in (a_old_col, s_old_row)])
        facts = FACTOR_DECAY * olds + keep * inv_rows * sums
        grad_mat = grad_mat.reshape(HIDDEN, BLOCK) * inv_rows
        layer_id = data_id // 2
        stack_id = layer_id // 2
        is_col = lax.rem(layer_id, 2) == 0
        half_at = lax.rem(data_id, 2) * D_ROWS
        full_inv = jnp.where(is_col, *[lax.dynamic_slice(inv, (stack_id, half_at, 0), (1, D_ROWS, HIDDEN))[0] for inv in (a_inv_col, s_inv_row)])
        block_inv = jnp.where(is_col, *[lax.dynamic_slice(inv, (stack_id, 0, 0), (1, BLOCK, BLOCK))[0] for inv in (s_inv_col, a_inv_row)])
        u_half = exact_dot(exact_dot(full_inv, grad_mat), block_inv)
        old_blocks = jnp.concatenate([lax.dynamic_slice(old, (0, 32 * data_id, 0), (2, 32, BLOCK)) for old in (s_old_col, a_old_row)])
        new_blocks = jnp.swapaxes(share[BLOCK_BASE:].reshape(2, 2, 32, BLOCK), 0, 1).reshape(4, 32, BLOCK)
        blocks = FACTOR_DECAY * old_blocks + keep * inv_rows * new_blocks
        fact_all, u_all, blk_all = gather_results(facts, u_half, blocks)
        u_all = u_all.reshape(2, 2, HIDDEN, BLOCK)
        u_col = u_all[:, 0]
        u_row = jnp.swapaxes(u_all[:, 1], 1, 2)
        return (u_col, u_row, fact_all[:2], blk_all[:2], blk_all[2:], fact_all[2:])

    batch_split = P('data', None)
    col_split = P(None, None, 'model')
    row_split = P(None, 'model', None)
    replicated = P()
    return jax.shard_map(
        shard_body,
        mesh=mesh,
        in_specs=(batch_split, batch_split, col_split, row_split, replicated, row_split, row_split, replicated, replicated, row_split, row_split, replicated),
        out_specs=(col_split, row_split, replicated, row_split, row_split, replicated),
        check_vma=False,
    )
```

time: 502 us -> 432 us (0.86)
  the two profiles are of different devices: /device:TPU:0 before, /device:TPU:9 now
where the time goes in v3:
time: 432 us; the launch traced here: 426 us
  Pallas kernels  348 us (81%)
  matrix products  45.9 us (11%)
  local copies, waits for them, and re-layouts  26.8 us (6%)
    pallas_call x1, Pallas kernels, scatter_call(): pl.pallas_call(functools.partial(scatter_kernel, rows), out_shape=[jax.Sh...  173 us
    pallas_call x2, Pallas kernels, gather_call(): pl.pallas_call(functools.partial(gather_kernel, Plan(len(args), items, or...  148 us
    pallas_call x1, Pallas kernels, gram_call(): pl.pallas_call(gram_kernel, out_shape=jax.ShapeDtypeStruct((32, SHARE_ROW...  26.8 us
    dot_general x3, matrix products, matmul(): return jnp.dot(left_mat, right_mat, preferred_element_type=jnp.float32)  14.4 us
    dot_general x3, matrix products, matmul_nt(): lax.dot_general(left_mat, right_mat, NT_DIMS, preferred_element_type=jnp....  14.1 us
    dot_general x2, matrix products, matmul_tn(): lax.dot_general(left_mat, right_mat, TN_DIMS, preferred_element_type=jnp....  12.8 us
    slice x2, local copies, waits for them, and re-layouts, shard_body(): return (u_col, u_row, fact_all[:2], blk_all[:2], blk_all[2:], fact_all[2:])  12.1 us

profile of v3, /device:TPU:9, one launch (start us, length us, event | category | flops | bytes accessed | tf_op | source)
XLA Modules:
  0.0 425.8 jit_solution(10687423084136113044)
XLA Ops:
  0.7 2.8 constant_dynamic-slice_fusion.2
  3.5 43.9 %weights.1 = (bf16[1024,1024]{1,0:T(8,128)(2,1)S(1)}, bf16[1024,1024]{1,0:T(8,128)(2,1)S(1)}, bf16[1024,1024]{1,0:T(8,128)(2,1)S(1)}, bf16[1024,1024]{1,0:T(8,128)(2,1)S(1)}) custom-call(bf16[2,1024,256]{2,1,0:T(8,128)(2,1)S(1)} %copy-done.1, bf16[2,256,1024]{2,1,0:T(8,128)(2,1)S(1)} %copy-done.2), custom_call_target="tpu_custom_call" | custom-call | flops 49999998976 | bytes 8388608 | tf_op jit(solution)/shard_map/weights/pallas_call | solution.py:321
  47.4 4.4 %fusion.18 = (bf16[1024,1024]{1,0:T(8,128)(2,1)}, bf16[1024,1024]{1,0:T(8,128)(2,1)S(1)}) fusion(bf16[1024,1024]{1,0:T(8,128)(2,1)S(1)} %get-tuple-element.46.x_ref, bf16[1024,1024]{1,0:T(8,128)(2,1)S(1)} %get-tuple-element.17), kind=kOutput, calls=%fused_computation.39 | convolution fusion | flops 2159017984 | bytes 8388608 | tf_op jit(solution)/shard_map/dot_general | solution.py:39
  51.8 5.1 %fusion.12 = (bf16[1024,1024]{1,0:T(8,128)(2,1)}, bf16[1024,1024]{1,0:T(8,128)(2,1)S(1)}) fusion(bf16[1024,1024]{1,0:T(8,128)(2,1)S(1)} %get-tuple-element.18, bf16[1024,1024]{1,0:T(8,128)(2,1)S(1)} %get-tuple-element.38), kind=kOutput, calls=%fused_computation.33 | convolution fusion | flops 2169503744 | bytes 8388608 | tf_op jit(solution)/shard_map/dot_general | solution.py:39
  56.8 4.9 %fusion.11 = (bf16[1024,1024]{1,0:T(8,128)(2,1)}, bf16[1024,1024]{1,0:T(8,128)(2,1)S(1)}) fusion(bf16[1024,1024]{1,0:T(8,128)(2,1)S(1)} %get-tuple-element.19, bf16[1024,1024]{1,0:T(8,128)(2,1)S(1)} %get-tuple-element.40), kind=kOutput, calls=%fused_computation.32 | convolution fusion | flops 2169503744 | bytes 8388608 | tf_op jit(solution)/shard_map/dot_general | solution.py:39
  61.8 0.0 copy-done.3
  61.8 4.7 %fusion.10.g3_ref = bf16[1024,1024]{1,0:T(8,128)(2,1)S(1)} fusion(bf16[1024,1024]{1,0:T(8,128)(2,1)S(1)} %get-tuple-element.42, bf16[1024,1024]{1,0:T(8,128)(2,1)S(1)} %get-tuple-element.45.dy_ref, bf16[1024,1024]{1,0:T(8,128)(2,1)S(1)} %get-tuple-element.16), kind=kOutput, calls=%fused_computation.31 | convolution fusion | flops 2170552320 | bytes 8388608 | tf_op jit(solution)/shard_map/dot_general | solution.py:47
  66.5 4.7 %fusion.17.g2_ref = bf16[1024,1024]{1,0:T(8,128)(2,1)S(1)} fusion(bf16[1024,1024]{1,0:T(8,128)(2,1)S(1)} %get-tuple-element.40, bf16[1024,1024]{1,0:T(8,128)(2,1)S(1)} %fusion.10.g3_ref, bf16[1024,1024]{1,0:T(8,128)(2,1)S(1)} %get-tuple-element.19), kind=kOutput, calls=%fused_computation.38 | convolution fusion | flops 2170552320 | bytes 8388608 | tf_op jit(solution)/shard_map/dot_general | solution.py:47
  71.2 0.0 copy-start.8
  71.2 4.7 %fusion.23.g1_ref = bf16[1024,1024]{1,0:T(8,128)(2,1)S(1)} fusion(bf16[1024,1024]{1,0:T(8,128)(2,1)S(1)} %get-tuple-element.38, bf16[1024,1024]{1,0:T(8,128)(2,1)S(1)} %fusion.17.g2_ref, bf16[1024,1024]{1,0:T(8,128)(2,1)S(1)} %get-tuple-element.18), kind=kOutput, calls=%fused_computation.44 | convolution fusion | flops 2170552320 | bytes 8388608 | tf_op jit(solution)/shard_map/dot_general | solution.py:47
  75.9 26.8 %gram.1 = f32[32,896,256]{2,1,0:T(8,128)} custom-call(bf16[1024,1024]{1,0:T(8,128)(2,1)S(1)} %get-tuple-element.46.x_ref, bf16[1024,1024]{1,0:T(8,128)(2,1)S(1)} %fusion.23.g1_ref, bf16[1024,1024]{1,0:T(8,128)(2,1)} %copy-done.8, bf16[1024,1024]{1,0:T(8,128)(2,1)} %get-tuple-element.37.h1_ref, bf16[1024,1024]{1,0:T(8,128)(2,1)} %get-tuple-element.39.h2_ref, ...), custom_call_target="tpu_custom_call" | custom-call | flops 15000000512 | bytes 46000000 | tf_op jit(solution)/shard_map/gram/pallas_call | solution.py:125
  102.7 6.4 %fusion.42 = f32[1024,256]{0,1:T(8,128)S(1)} fusion(bf16[4096,1024]{1,0:T(8,128)(2,1)} %param.12, s32[]{:T(128)S(6)} %select_n.59), kind=kOutput, calls=%fused_computation.68 | convolution fusion | flops 2147483648 | bytes 11534340 | tf_op jit(solution)/shard_map/dot_general | solution.py:43
  109.1 0.3 copy.18
  109.4 6.4 %fusion.45 = f32[1024,256]{0,1:T(8,128)S(1)} fusion(bf16[4096,1024]{1,0:T(8,128)(2,1)} %param.13, s32[]{:T(128)S(6)} %select_n.59), kind=kOutput, calls=%fused_computation.69 | convolution fusion | flops 2147483648 | bytes 11534340 | tf_op jit(solution)/shard_map/dot_general | solution.py:43
  115.8 0.3 copy.19
  116.2 1.5 pad_maximum_fusion.ends_ref
  117.7 172.9 %sums.1 = (f32[896,256]{1,0:T(8,128)}, f32[2,128,256]{2,1,0:T(8,128)}, f32[2,512,256]{2,1,0:T(8,128)}) custom-call(f32[4,2,2,2,896,256]{5,4,3,2,1,0:T(8,128)} %bitcast.51, f32[2,2,2,2,128,256]{5,4,3,2,1,0:T(8,128)} %pad_maximum_fusion.ends_ref), custom_call_target="tpu_custom_call" | custom-call | flops 120000004096 | bytes 62914560 | tf_op jit(solution)/shard_map/sums/pallas_call | solution.py:573
  290.6 0.0 copy-start.5
  290.7 0.0 copy-start.6
  290.7 1.4 broadcast_multiply_fusion
  292.1 4.1 fusion.33
  296.2 0.6 fusion.50.refs_1_
  296.8 1.1 slice_multiply_fusion
  297.9 1.1 constant_dynamic-slice_fusion.4
  299.0 0.1 fusion.49.refs_0_
  299.1 0.9 constant_dynamic-slice_fusion
  300.0 104.0 %results.1 = (f32[4,1024,1024]{2,1,0:T(8,128)S(1)}, f32[8,512,256]{2,1,0:T(8,128)S(1)}, f32[4,256,256]{2,1,0:T(8,128)S(1)}) custom-call(f32[4,128,256]{2,1,0:T(8,128)S(1)} %fusion.49.refs_0_, f32[512,256]{1,0:T(8,128)S(1)} %fusion.50.refs_1_, f32[4,32,256]{2,1,0:T(8,128)S(1)} %fusion.55.refs_2_), custom_call_target="tpu_custom_call" | custom-call | flops 49999998976 | bytes 22020096 | tf_op jit(solution)/shard_map/results/pallas_call | solution.py:321
  404.0 5.7 %copy-done = f32[4,1024,1024]{2,1,0:T(8,128)} copy-done((f32[4,1024,1024]{2,1,0:T(8,128)}, f32[4,1024,1024]{2,1,0:T(8,128)S(1)}, u32[]{:S(2)}) %copy-start) | copy-done | bytes 16777240
  409.7 11.0 %fusion.63 = (f32[2,1024,1024]{2,1,0:T(8,128)}, f32[2,1024,1024]{2,1,0:T(8,128)}) fusion(f32[4,1024,1024]{2,1,0:T(8,128)} %copy-done), kind=kLoop, calls=%fused_computation.96 | loop fusion | bytes 33554432 | tf_op jit(solution)/shard_map/slice | solution.py:635
  420.8 1.7 fusion.64
  422.5 1.8 copy.24
  424.3 1.0 fusion.65
  (16 shorter events, 0.1 us)
Async XLA Ops:
  0.6 2.8 copy-start.1
  0.6 2.8 copy-start.2
  3.5 58.3 %copy-start.3 = (bf16[1024,1024]{1,0:T(8,128)(2,1)}, bf16[1024,1024]{1,0:T(8,128)(2,1)S(1)}, u32[]{:S(2)}) copy-start(bf16[1024,1024]{1,0:T(8,128)(2,1)S(1)} %get-tuple-element.45.dy_ref) | copy-start | bytes 6291460
  66.4 4.7 %copy-start.7 = (bf16[1024,1024]{1,0:T(8,128)(2,1)}, bf16[1024,1024]{1,0:T(8,128)(2,1)S(1)}, u32[]{:S(2)}) copy-start(bf16[1024,1024]{1,0:T(8,128)(2,1)S(1)} %fusion.10.g3_ref) | copy-start | bytes 6291460
  71.2 4.7 %copy-start.8 = (bf16[1024,1024]{1,0:T(8,128)(2,1)}, bf16[1024,1024]{1,0:T(8,128)(2,1)S(1)}, u32[]{:S(2)}) copy-start(bf16[1024,1024]{1,0:T(8,128)(2,1)S(1)} %fusion.17.g2_ref) | copy-start | bytes 6291460
  290.6 5.5 %copy-start.5 = (f32[2,256,256]{2,1,0:T(8,128)S(1)}, f32[2,256,256]{2,1,0:T(8,128)}, u32[]{:S(2)}) copy-start(f32[2,256,256]{2,1,0:T(8,128)} %param.22) | copy-start | bytes 1572868
  290.7 5.5 %copy-start.6 = (f32[2,256,256]{2,1,0:T(8,128)S(1)}, f32[2,256,256]{2,1,0:T(8,128)}, u32[]{:S(2)}) copy-start(f32[2,256,256]{2,1,0:T(8,128)} %param.21) | copy-start | bytes 1572868
  292.0 5.8 %copy-start.4 = (f32[2,128,256]{2,1,0:T(8,128)S(1)}, f32[2,128,256]{2,1,0:T(8,128)}, u32[]{:S(2)}) copy-start(f32[2,128,256]{2,1,0:T(8,128)} %get-tuple-element.20) | copy-start | bytes 786436
  404.0 5.7 %copy-start = (f32[4,1024,1024]{2,1,0:T(8,128)}, f32[4,1024,1024]{2,1,0:T(8,128)S(1)}, u32[]{:S(2)}) copy-start(f32[4,1024,1024]{2,1,0:T(8,128)S(1)} %get-tuple-element.24) | copy-start | bytes 50331652

commit v4 on v3

--- a/solution.py
+++ b/solution.py
@@ -55,23 +55,29 @@
 BLOCK = 256
 HIDDEN = 1024
 D_ROWS = 512
+SYM_ROWS = 80
 FULL_BASE = 512
-BLOCK_BASE = 768
-SHARE_ROWS = 896
+BLOCK_BASE = 672
+SHARE_ROWS = 800
+LANES = 128
+STRIP = 32
+HALF_STRIP = 16
+CORES = 8
 
 
 def gram_kernel(x_ref, g1_ref, g2_ref, h1_ref, h2_ref, g3_ref, dy_ref, h3_ref, out_ref,
-                act, stage, bstage, in_sem, out_sem, b_sem):
+                act, stage, bstage, fstage, in_sem, out_sem, b_sem, f_sem):
     sources = [dy_ref, h3_ref, h2_ref, g3_ref, g2_ref, h1_ref, x_ref, g1_ref]
     slots = [3, 7, 2, 6, 1, 5, 0, 4]
     loads = [pltpu.make_async_copy(src, act.at[slot], in_sem.at[slot]) for src, slot in zip(sources, slots)]
     for load in loads:
         load.start()
-    started = [0]
-    pend = {}
 
     def out_copy(slot, dst):
         return pltpu.make_async_copy(stage.at[slot], dst, out_sem.at[slot])
+
+    def f_copy(slot, n, which):
+        return pltpu.make_async_copy(fstage.at[slot], out_ref.at[pl.ds(n * CORES, CORES), pl.ds(FULL_BASE + which * SYM_ROWS, SYM_ROWS)], f_sem.at[slot])
 
     for layer in (3, 2, 1, 0):
         pltpu.make_async_copy(x_ref, act.at[layer], in_sem.at[layer]).wait()
@@ -81,22 +87,22 @@
             slot = lax.rem(m, 2)
             cols = pl.ds(pl.multiple_of(m * BLOCK, BLOCK), BLOCK)
             right = act[4 + layer, :, cols]
-            dst = out_ref.at[pl.ds(m * 8 + 2 * layer, 2), pl.ds(0, D_ROWS)]
+            dst = out_ref.at[pl.ds(m * CORES + 2 * layer, 2), pl.ds(0, D_ROWS)]
 
             if layer == 3:
                 @pl.when(m >= 2)
                 def _():
                     out_copy(slot, dst).wait()
-                    pltpu.make_async_copy(bstage.at[slot], out_ref.at[pl.ds(0, 8), pl.ds(BLOCK_BASE, 32)], b_sem.at[slot]).wait()
+                    pltpu.make_async_copy(bstage.at[slot], out_ref.at[pl.ds(0, CORES), pl.ds(BLOCK_BASE, STRIP)], b_sem.at[slot]).wait()
             else:
                 out_copy(slot, dst).wait()
-                pltpu.make_async_copy(bstage.at[slot], out_ref.at[pl.ds(0, 8), pl.ds(BLOCK_BASE, 32)], b_sem.at[slot]).wait()
+                pltpu.make_async_copy(bstage.at[slot], out_ref.at[pl.ds(0, CORES), pl.ds(BLOCK_BASE, STRIP)], b_sem.at[slot]).wait()
             prod = lax.dot_general(act[layer], right, TN_DIMS, preferred_element_type=jnp.float32)
             stage[slot] = prod.reshape(2, D_ROWS, BLOCK)
             out_copy(slot, dst).start()
             blk = lax.dot_general(right, right, TN_DIMS, preferred_element_type=jnp.float32)
-            bstage[slot] = blk.reshape(8, 32, BLOCK)
-            pltpu.make_async_copy(bstage.at[slot], out_ref.at[pl.ds(m * 8, 8), pl.ds(BLOCK_BASE + 32 * layer, 32)], b_sem.at[slot]).start()
+            bstage[slot] = blk.reshape(CORES, STRIP, BLOCK)
+            pltpu.make_async_copy(bstage.at[slot], out_ref.at[pl.ds(m * CORES, CORES), pl.ds(BLOCK_BASE + STRIP * layer, STRIP)], b_sem.at[slot]).start()
             return carry
 
         lax.fori_loop(0, 4, d_body, 0)
@@ -106,32 +112,35 @@
 
             def f_body(n, carry, layer=layer, which=which):
                 slot = lax.rem(n, 2)
-                cols = pl.ds(pl.multiple_of(n * BLOCK, BLOCK), BLOCK)
-                dst = out_ref.at[pl.ds(n * 8, 8), pl.ds(FULL_BASE + which * 128, 128)]
-                pltpu.make_async_copy(stage.at[slot], out_ref.at[pl.ds(0, 2), pl.ds(0, D_ROWS)], out_sem.at[slot]).wait()
-                prod = lax.dot_general(act[layer], act[layer, :, cols], TN_DIMS, preferred_element_type=jnp.float32)
-                stage[slot] = prod.reshape(2, D_ROWS, BLOCK)
-                pltpu.make_async_copy(stage.at[slot].reshape(8, 128, BLOCK), dst, out_sem.at[slot]).start()
+                if which == 0:
+                    pl.when(n >= 2)(lambda: f_copy(slot, n, which).wait())
+                else:
+                    f_copy(slot, n, which).wait()
+                put_sym(fstage.at[slot], sym_blocks(act.at[layer], n), False)
+                f_copy(slot, n, which).start()
                 return carry
 
             lax.fori_loop(0, 4, f_body, 0)
     for slot in range(2):
+        f_copy(slot, 0, 0).wait()
         pltpu.make_async_copy(stage.at[slot], out_ref.at[pl.ds(0, 2), pl.ds(0, D_ROWS)], out_sem.at[slot]).wait()
-        pltpu.make_async_copy(bstage.at[slot], out_ref.at[pl.ds(0, 8), pl.ds(BLOCK_BASE, 32)], b_sem.at[slot]).wait()
+        pltpu.make_async_copy(bstage.at[slot], out_ref.at[pl.ds(0, CORES), pl.ds(BLOCK_BASE, STRIP)], b_sem.at[slot]).wait()
 
 
 def gram_call(x_loc, g_one, g_two, h_one, h_two, g_three, dy_loc, h_three):
     any_spec = pl.BlockSpec(memory_space=pl.ANY)
     return pl.pallas_call(
         gram_kernel,
-        out_shape=jax.ShapeDtypeStruct((32, SHARE_ROWS, BLOCK), jnp.float32),
-        in_specs=[any_spec] * 8,
+        out_shape=jax.ShapeDtypeStruct((STRIP, SHARE_ROWS, BLOCK), jnp.float32),
+        in_specs=[any_spec] * CORES,
         out_specs=any_spec,
         scratch_shapes=[
-            pltpu.VMEM((8, HIDDEN, HIDDEN), jnp.bfloat16),
+            pltpu.VMEM((CORES, HIDDEN, HIDDEN), jnp.bfloat16),
             pltpu.VMEM((2, 2, D_ROWS, BLOCK), jnp.float32),
-            pltpu.VMEM((2, 8, 32, BLOCK), jnp.float32),
-            pltpu.SemaphoreType.DMA((8,)),
+            pltpu.VMEM((2, CORES, STRIP, BLOCK), jnp.float32),
+            pltpu.VMEM((2, CORES, SYM_ROWS, BLOCK), jnp.float32),
+            pltpu.SemaphoreType.DMA((CORES,)),
+            pltpu.SemaphoreType.DMA((2,)),
             pltpu.SemaphoreType.DMA((2,)),
             pltpu.SemaphoreType.DMA((2,)),
         ],
@@ -142,7 +151,7 @@
 
 
 MESH_ID = pl.DeviceIdType.MESH
-CHUNK_ORDER = ((0, 0), (3, 0), (0, 1), (3, 1), (1, 0), (2, 0), (1, 1), (2, 1))
+CHUNK_ORDER = tuple((zd, h) for pair in ((0, 3), (1, 2)) for h in range(2) for zd in pair)
 
 
 def torus_place():
@@ -151,7 +160,7 @@
     y = d // 4
     x = (d // 2) % 2
     c = d % 2
-    near = {'x': (z, d + 2 - 4 * x), 'y': (z, d + 4 - 8 * y), 'c': (z, d + 1 - 2 * c), 'up': (z + 1, d), 'dn': (z - 1, d)}
+    near = {'x': (z, d + 2 - 4 * x), 'y': (z, d + 4 - CORES * y), 'c': (z, d + 1 - 2 * c), 'up': (z + 1, d), 'dn': (z - 1, d)}
     return z, y, x, c, near
 
 
@@ -174,10 +183,36 @@
     return pltpu.make_async_remote_copy(src_ref=src, dst_ref=dst, send_sem=send_sem, recv_sem=recv_sem, device_id=where, device_id_type=MESH_ID)
 
 
+def sym_blocks(left, n):
+    def cols(at, size):
+        return left[:, pl.ds(pl.multiple_of(at, LANES), size)]
+
+    low = n % 2
+    right = cols(n * BLOCK, BLOCK)
+    pairs = ((right, right, STRIP), (cols((n + 1) % 4 * BLOCK, BLOCK), right, STRIP),
+             (cols((low + 2) * BLOCK + n // 2 * LANES, LANES), cols(low * BLOCK, BLOCK), HALF_STRIP))
+    return [lax.dot_general(a, b, TN_DIMS, preferred_element_type=jnp.float32).reshape(CORES, rows, BLOCK) for a, b, rows in pairs]
+
+
+def put_sym(dst, blocks, more):
+    at = 0
+    for blk in blocks:
+        span = pl.ds(at, blk.shape[1])
+        dst[:, span] = dst[:, span] + blk if more else blk
+        at += blk.shape[1]
+
+
 def gather_kernel(plan, *refs):
     n = len(plan.items)
-    pieces, outs, lands = refs[:plan.n_in], refs[plan.n_in:plan.n_in + n], refs[plan.n_in + n:plan.n_in + 2 * n]
-    load_sem, z_recv, x_recv, y_recv, d_recv, c_recv, up_send, dn_send, x_send, y_send, dy_send, dx_send, c_send, flush_sem = refs[plan.n_in + 2 * n:]
+    pieces, refs = refs[:plan.n_in], refs[plan.n_in:]
+    outs, refs = refs[:n], refs[n:]
+    ends = len(plan.tokens) > 0
+    if ends:
+        ends_ref, refs = refs[0], refs[1:]
+    lands, refs = refs[:n], refs[n:]
+    if ends:
+        tok, acc, tok_sem, acc_sem, *refs = refs
+    load_sem, z_recv, x_recv, y_recv, d_recv, c_recv, up_send, dn_send, x_send, y_send, dy_send, dx_send, c_send, flush_sem = refs
     z, y, x, c, near = torus_place()
 
     def slot(ref, j, zs, yy, xx, cc):
@@ -195,6 +230,26 @@
     loads = [pltpu.make_async_copy(item.piece(pieces, z, 4 * y + 2 * x + c), view(j, z, y, x, c), load_sem.at[j]) for j, item in enumerate(plan.items)]
     for load in loads:
         load.start()
+
+    def tok_load(t):
+        src = pieces[plan.tokens[t // 4]].at[pl.ds(t % 4 * HIDDEN, HIDDEN)]
+        return pltpu.make_async_copy(src, tok.at[t % 2], tok_sem.at[t % 2])
+
+    def ends_out(mat):
+        return pltpu.make_async_copy(acc.at[mat], ends_ref.at[mat], acc_sem.at[mat])
+
+    def ends_step(t):
+        tok_load(t).wait()
+        put_sym(acc.at[t // 4], sym_blocks(tok.at[t % 2], z), t % 4 > 0)
+        if t + 2 < CORES:
+            tok_load(t + 2).start()
+        if t % 4 == 3:
+            ends_out(t // 4).start()
+
+    todo = list(range(CORES)) if ends else []
+    if ends:
+        tok_load(0).start()
+        tok_load(1).start()
     meet_neighbours(z, near)
 
     def side_copy(j, zs, side):
@@ -297,6 +352,13 @@
             if 0 <= step - lag < 4:
                 for j, off in waves[step - lag]:
                     func(j, off)
+                if todo:
+                    ends_step(todo.pop(0))
+    for t in todo:
+        ends_step(t)
+    if ends:
+        ends_out(0).wait()
+        ends_out(1).wait()
     for wave in waves:
         for j, off in wave:
             last_step(j, off)
@@ -308,70 +370,75 @@
 
 
 class Plan:
-    def __init__(self, n_in, items, order):
-        self.n_in, self.items, self.order = n_in, items, order
-
-
-def gather_call(args, items, order, collective_id, name):
+    def __init__(self, n_in, items, order, tokens):
+        self.n_in, self.items, self.order, self.tokens = n_in, items, order, tokens
+
+
+def gather_call(args, items, order, collective_id, name, tokens=()):
     n = len(items)
     dma = pltpu.SemaphoreType.DMA
     size = sum(math.prod(item.shape) * jnp.dtype(item.dtype).itemsize for item in items)
     hbm = pl.BlockSpec(memory_space=pltpu.HBM)
     flat = dma((n, 4))
+    shapes = [jax.ShapeDtypeStruct(item.shape, item.dtype) for item in items]
+    extra = []
+    if tokens:
+        part = (2, CORES, SYM_ROWS, BLOCK)
+        shapes.append(jax.ShapeDtypeStruct(part, jnp.float32))
+        extra = [pltpu.VMEM((2, HIDDEN, HIDDEN), jnp.bfloat16), pltpu.VMEM(part, jnp.float32), dma((2,)), dma((2,))]
     return pl.pallas_call(
-        functools.partial(gather_kernel, Plan(len(args), items, order)),
-        out_shape=[jax.ShapeDtypeStruct(item.shape, item.dtype) for item in items],
+        functools.partial(gather_kernel, Plan(len(args), items, order, tokens)),
+        out_shape=shapes,
         in_specs=[hbm] * len(args),
-        out_specs=[hbm] * n,
-        scratch_shapes=[pltpu.VMEM(item.shape, item.dtype) for item in items]
-        + [dma((n,)), flat, flat, flat, dma((n, 4, 2)), dma((n, 4, 4)), flat, flat, flat, flat, flat, flat, dma((n, 4, 4)), dma((n, 4, 8))],
-        compiler_params=pltpu.CompilerParams(collective_id=collective_id, has_side_effects=True, vmem_limit_bytes=size + 8 * MIB),
+        out_specs=[hbm] * len(shapes),
+        scratch_shapes=[pltpu.VMEM(item.shape, item.dtype) for item in items] + extra
+        + [dma((n,)), flat, flat, flat, dma((n, 4, 2)), dma((n, 4, 4)), flat, flat, flat, flat, flat, flat, dma((n, 4, 4)), dma((n, 4, CORES))],
+        compiler_params=pltpu.CompilerParams(collective_id=collective_id, has_side_effects=True, vmem_limit_bytes=size + HALF_STRIP * MIB),
         cost_estimate=pl.CostEstimate(flops=50_000_000_000, bytes_accessed=size, transcendentals=0),
         name=name,
     )(*args)
 
 
 def col_slot(ref, zs, d):
-    return ref.at[pl.ds(d * 128, 128), pl.ds(zs * BLOCK, BLOCK)]
+    return ref.at[pl.ds(d * LANES, LANES), pl.ds(zs * BLOCK, BLOCK)]
 
 
 def col_half(ref, zs, d, which):
-    return ref.at[pl.ds(d * 128 + which * 64, 64), pl.ds(zs * BLOCK, BLOCK)]
+    return ref.at[pl.ds(d * LANES + which * 64, 64), pl.ds(zs * BLOCK, BLOCK)]
 
 
 def row_slot(ref, zs, d):
-    return ref.at[pl.ds((zs * 8 + d) * 32, 32)]
+    return ref.at[pl.ds((zs * CORES + d) * STRIP, STRIP)]
 
 
 def row_half(ref, zs, d, which):
-    return ref.at[pl.ds((zs * 8 + d) * 32 + which * 16, 16)]
-
-
-def gather_weights(w_col, w_row):
+    return ref.at[pl.ds((zs * CORES + d) * STRIP + which * HALF_STRIP, HALF_STRIP)]
+
+
+def gather_weights(w_col, w_row, x_tokens, dy_tokens):
     shape = (HIDDEN, HIDDEN)
-    items = [Item(shape, w_col.dtype, lambda refs, z, d, i=i: refs[0].at[i, pl.ds(d * 128, 128)], col_slot, col_half) for i in range(2)]
-    items += [Item(shape, w_row.dtype, lambda refs, z, d, i=i: refs[1].at[i, pl.ds(d * 32, 32)], row_slot, row_half) for i in range(2)]
-    return gather_call((w_col, w_row), items, (0, 3, 2, 1), 1, 'weights')
+    items = [Item(shape, w_col.dtype, lambda refs, z, d, i=i: refs[0].at[i, pl.ds(d * LANES, LANES)], col_slot, col_half) for i in range(2)]
+    items += [Item(shape, w_row.dtype, lambda refs, z, d, i=i: refs[1].at[i, pl.ds(d * STRIP, STRIP)], row_slot, row_half) for i in range(2)]
+    return gather_call((w_col, w_row, x_tokens, dy_tokens), items, (0, 3, 2, 1), 1, 'weights', (2, 3))
 
 
 def gather_results(facts, u_half, blocks):
     items = [
-        Item((4, HIDDEN, HIDDEN), facts.dtype, lambda refs, z, d: refs[0],
-             lambda ref, zs, d: ref.at[:, pl.ds(d * 128, 128), pl.ds(zs * BLOCK, BLOCK)],
-             lambda ref, zs, d, which: ref.at[pl.ds(2 * which, 2), pl.ds(d * 128, 128), pl.ds(zs * BLOCK, BLOCK)]),
-        Item((8, D_ROWS, BLOCK), facts.dtype, lambda refs, z, d: refs[1],
+        Item((STRIP, 4, SYM_ROWS, BLOCK), facts.dtype, lambda refs, z, d: refs[0],
+             lambda ref, zs, d: ref.at[zs * CORES + d], lambda ref, zs, d, which: ref.at[zs * CORES + d, pl.ds(2 * which, 2)]),
+        Item((CORES, D_ROWS, BLOCK), facts.dtype, lambda refs, z, d: refs[1],
              lambda ref, zs, d: ref.at[d], lambda ref, zs, d, which: ref.at[d, pl.ds(which * BLOCK, BLOCK)], True),
         Item((4, BLOCK, BLOCK), facts.dtype, lambda refs, z, d: refs[2],
-             lambda ref, zs, d: ref.at[:, pl.ds(d * 32, 32)], lambda ref, zs, d, which: ref.at[pl.ds(2 * which, 2), pl.ds(d * 32, 32)], True),
+             lambda ref, zs, d: ref.at[:, pl.ds(d * STRIP, STRIP)], lambda ref, zs, d, which: ref.at[pl.ds(2 * which, 2), pl.ds(d * STRIP, STRIP)], True),
     ]
     return gather_call((facts, u_half, blocks), items, (1, 2, 0), 3, 'results')
 
 
 def add_into(dst, src, rows):
-    step = 32 if rows % 32 == 0 else 16 if rows % 16 == 0 else 8
+    step = max(n for n in range(CORES, 65, CORES) if rows % n == 0)
 
     def body(i, carry):
-        span = pl.ds(pl.multiple_of(i * step, 8), step)
+        span = pl.ds(pl.multiple_of(i * step, CORES), step)
         dst[span, :] = dst[span, :] + src[span, :]
         return carry
 
@@ -500,23 +567,23 @@
         for mat in range(2):
             for yy in range(2):
                 for xx in range(2):
-                    add_into(eown.at[mat, yy, xx], emate.at[mat, yy, xx], 128)
+                    add_into(eown.at[mat, yy, xx], emate.at[mat, yy, xx], SYM_ROWS)
             eones[mat].start()
 
     def ends_b():
         eones[0].wait_recv()
         for yy in range(2):
-            add_into(eown.at[0, yy, x], eone.at[0, yy], 128)
+            add_into(eown.at[0, yy, x], eone.at[0, yy], SYM_ROWS)
         etwos[0].start()
         eones[1].wait_recv()
         for xx in range(2):
-            add_into(eown.at[1, y, xx], eone.at[1, xx], 128)
+            add_into(eown.at[1, y, xx], eone.at[1, xx], SYM_ROWS)
         etwos[1].start()
 
     def ends_c():
         for mat in range(2):
             etwos[mat].wait_recv()
-            add_into(eown.at[mat, y, x], etwo.at[mat], 128)
+            add_into(eown.at[mat, y, x], etwo.at[mat], SYM_ROWS)
             pltpu.make_async_copy(eown.at[mat, y, x], eshare_ref.at[mat], out2_sem.at[mat]).start()
 
     n = len(CHUNK_ORDER)
@@ -568,21 +635,59 @@
     one_buf = pltpu.VMEM((4, 2, half, BLOCK), f32)
     two_buf = pltpu.VMEM((4, half, BLOCK), f32)
     z_buf = pltpu.VMEM((4, rows, BLOCK), f32)
-    e_buf = pltpu.VMEM((2, 2, 2, 128, BLOCK), f32)
+    e_buf = pltpu.VMEM((2, 2, 2, SYM_ROWS, BLOCK), f32)
     hbm = pl.BlockSpec(memory_space=pltpu.HBM)
     return pl.pallas_call(
         functools.partial(scatter_kernel, rows),
-        out_shape=[jax.ShapeDtypeStruct((rows, BLOCK), f32), jax.ShapeDtypeStruct((2, 128, BLOCK), f32), jax.ShapeDtypeStruct((2, D_ROWS, BLOCK), f32)],
+        out_shape=[jax.ShapeDtypeStruct((rows, BLOCK), f32), jax.ShapeDtypeStruct((2, SYM_ROWS, BLOCK), f32), jax.ShapeDtypeStruct((2, D_ROWS, BLOCK), f32)],
         in_specs=[hbm] * 2,
         out_specs=[hbm] * 3,
         scratch_shapes=[whole, whole, one_buf, one_buf, two_buf, two_buf, z_buf, z_buf,
-                        e_buf, e_buf, pltpu.VMEM((2, 2, 128, BLOCK), f32), pltpu.VMEM((2, 128, BLOCK), f32), pltpu.VMEM((D_ROWS, BLOCK), f32),
+                        e_buf, e_buf, pltpu.VMEM((2, 2, SYM_ROWS, BLOCK), f32), pltpu.VMEM((2, SYM_ROWS, BLOCK), f32), pltpu.VMEM((D_ROWS, BLOCK), f32),
                         dma((1,)), dma((2,)), dma((4,)), dma((4,)), dma((2,)), dma((4,))]
-        + [dma((n, 2))] * 3 + [dma((n,))] * 8 + [dma((n, 2))] * 4 + [dma((2, 2))],
+        + [dma((n, 2))] * 3 + [dma((n,))] * CORES + [dma((n, 2))] * 4 + [dma((2, 2))],
         compiler_params=pltpu.CompilerParams(collective_id=collective_id, has_side_effects=True, vmem_limit_bytes=60 * MIB),
         cost_estimate=pl.CostEstimate(flops=120_000_000_000, bytes_accessed=60 * MIB, transcendentals=0),
         name=name,
-    )(parts.reshape(4, 2, 2, 2, rows, BLOCK), ends.reshape(2, 2, 2, 2, 128, BLOCK))
+    )(parts.reshape(4, 2, 2, 2, rows, BLOCK), ends.reshape(2, 2, 2, 2, SYM_ROWS, BLOCK))
+
+
+def mirror_kernel(in_ref, a_ref, s_ref):
+    def block(i, j, mat):
+        def take(plane, at, size):
+            return in_ref[plane, :, mat, pl.ds(at, size)].reshape(CORES * size, BLOCK)
+
+        if i == j:
+            return take(j, 0, STRIP)
+        if i == (j + 1) % 4:
+            return take(j, STRIP, STRIP)
+        if j == (i + 1) % 4:
+            return take(i, STRIP, STRIP).T
+        low = min(i, j)
+        both = jnp.concatenate([take(low, 64, HALF_STRIP), take(low + 2, 64, HALF_STRIP)], axis=0)
+        return both if i > j else both.T
+
+    for i in range(4):
+        @pl.when(pl.program_id(1) == i)
+        def _(i=i):
+            for mat, out in enumerate((a_ref, s_ref)):
+                for j in range(4):
+                    out[0, :, pl.ds(j * BLOCK, BLOCK)] = block(i, j, mat)
+
+
+def mirror_call(facts):
+    full = jax.ShapeDtypeStruct((2, HIDDEN, HIDDEN), facts.dtype)
+    out_spec = pl.BlockSpec((1, BLOCK, HIDDEN), lambda k, i: (k, i, 0))
+    return pl.pallas_call(
+        mirror_kernel,
+        grid=(2, 4),
+        out_shape=[full, full],
+        in_specs=[pl.BlockSpec((4, CORES, 2, SYM_ROWS, BLOCK), lambda k, i: (0, 0, k, 0, 0))],
+        out_specs=[out_spec, out_spec],
+        compiler_params=pltpu.CompilerParams(vmem_limit_bytes=STRIP * MIB),
+        cost_estimate=pl.CostEstimate(flops=10_000_000_000, bytes_accessed=26 * MIB, transcendentals=0),
+        name='mirror',
+    )(facts.reshape(4, CORES, 4, SYM_ROWS, BLOCK))
 
 
 def solution(mesh):
@@ -593,10 +698,7 @@
         model_id = lax.axis_index('model')
         data_id = lax.axis_index('data')
         inv_rows = 1.0 / (x_tokens.shape[0] * data_ways)
-        w_one, w_three, w_two, w_four = gather_weights(w_col, w_row)
-        x_cols = lax.dynamic_slice(x_tokens, (0, BLOCK * model_id), (x_tokens.shape[0], BLOCK))
-        dy_cols = lax.dynamic_slice(dy_tokens, (0, BLOCK * model_id), (x_tokens.shape[0], BLOCK))
-        ends = jnp.stack([matmul_tn(x_tokens, x_cols), matmul_tn(dy_tokens, dy_cols)])
+        w_one, w_three, w_two, w_four, ends = gather_weights(w_col, w_row, x_tokens, dy_tokens)
         rows_dev = x_tokens.shape[0] // model_ways
         x_loc = lax.dynamic_slice(x_tokens, (rows_dev * model_id, 0), (rows_dev, HIDDEN))
         dy_loc = lax.dynamic_slice(dy_tokens, (rows_dev * model_id, 0), (rows_dev, HIDDEN))
@@ -612,11 +714,14 @@
         parts = gram_call(x_loc, g_one, g_two, h_one, h_two, g_three, dy_loc, h_three)
         share, eshare, grad_mat = scatter_call(parts, ends, 2, 'sums')
         keep = 1.0 - FACTOR_DECAY
-        spot = (0, 128 * data_id, BLOCK * model_id)
-        mids = share[FULL_BASE:BLOCK_BASE].reshape(2, 128, BLOCK)
-        sums = jnp.stack([eshare[0], mids[0], mids[1], eshare[1]])
-        olds = jnp.concatenate([lax.dynamic_slice(old, spot, (2, 128, BLOCK)) for old in (a_old_col, s_old_row)])
-        facts = FACTOR_DECAY * olds + keep * inv_rows * sums
+        low = lax.rem(model_id, 2)
+        spots = ((model_id * BLOCK + STRIP * data_id, model_id * BLOCK, STRIP),
+                 (lax.rem(model_id + 1, 4) * BLOCK + STRIP * data_id, model_id * BLOCK, STRIP),
+                 ((low + 2) * BLOCK + model_id // 2 * LANES + HALF_STRIP * data_id, low * BLOCK, HALF_STRIP))
+        olds = [jnp.concatenate([lax.dynamic_slice(old, (0, at, col), (2, size, BLOCK)) for at, col, size in spots], axis=1) for old in (a_old_col, s_old_row)]
+        mids = share[FULL_BASE:BLOCK_BASE].reshape(2, SYM_ROWS, BLOCK)
+        sums = jnp.stack([eshare[0], mids[1], mids[0], eshare[1]])
+        facts = FACTOR_DECAY * jnp.stack(olds, axis=1).reshape(4, SYM_ROWS, BLOCK) + keep * inv_rows * sums
         grad_mat = grad_mat.reshape(HIDDEN, BLOCK) * inv_rows
         layer_id = data_id // 2
         stack_id = layer_id // 2
@@ -625,14 +730,15 @@
         full_inv = jnp.where(is_col, *[lax.dynamic_slice(inv, (stack_id, half_at, 0), (1, D_ROWS, HIDDEN))[0] for inv in (a_inv_col, s_inv_row)])
         block_inv = jnp.where(is_col, *[lax.dynamic_slice(inv, (stack_id, 0, 0), (1, BLOCK, BLOCK))[0] for inv in (s_inv_col, a_inv_row)])
         u_half = exact_dot(exact_dot(full_inv, grad_mat), block_inv)
-        old_blocks = jnp.concatenate([lax.dynamic_slice(old, (0, 32 * data_id, 0), (2, 32, BLOCK)) for old in (s_old_col, a_old_row)])
-        new_blocks = jnp.swapaxes(share[BLOCK_BASE:].reshape(2, 2, 32, BLOCK), 0, 1).reshape(4, 32, BLOCK)
+        old_blocks = jnp.concatenate([lax.dynamic_slice(old, (0, STRIP * data_id, 0), (2, STRIP, BLOCK)) for old in (s_old_col, a_old_row)])
+        new_blocks = jnp.swapaxes(share[BLOCK_BASE:].reshape(2, 2, STRIP, BLOCK), 0, 1).reshape(4, STRIP, BLOCK)
         blocks = FACTOR_DECAY * old_blocks + keep * inv_rows * new_blocks
         fact_all, u_all, blk_all = gather_results(facts, u_half, blocks)
+        a_new_col, s_new_row = mirror_call(fact_all)
         u_all = u_all.reshape(2, 2, HIDDEN, BLOCK)
         u_col = u_all[:, 0]
         u_row = jnp.swapaxes(u_all[:, 1], 1, 2)
-        return (u_col, u_row, fact_all[:2], blk_all[:2], blk_all[2:], fact_all[2:])
+        return (u_col, u_row, a_new_col, blk_all[:2], blk_all[2:], s_new_row)
 
     batch_split = P('data', None)
     col_split = P(None, None, 'model')

time: 432 us -> 382 us (0.88)
  Pallas kernels: 348 us -> 320 us
  matrix products: 45.9 us -> 32.9 us
  local copies, waits for them, and re-layouts: 26.8 us -> 19.4 us
    pallas_call x1, Pallas kernels: 173 us -> 154 us  [scatter_call(): pl.pallas_call(functools.partial(scatter_kernel, rows), out_shape=[jax.Sh...]
    pallas_call x2, Pallas kernels: 148 us -> 133 us  [gather_call(): pl.pallas_call(functools.partial(gather_kernel, Plan(len(args), items, or...]
    dot_general x2 -> x0, matrix products: 12.8 us -> none  [matmul_tn(): lax.dot_general(left_mat, right_mat, TN_DIMS, preferred_element_type=jnp....]
    slice x3, local copies, waits for them, and re-layouts: 12.1 us -> 1.99 us  [the longest x1 1.03 us: shard_body(): return (u_col, u_row, a_new_col, blk_all[:2], blk_all[2:], s_new_row)]
    pallas_call x1 -> x2, Pallas kernels: 26.8 us -> 32.7 us  [the longest x1 24.9 us: gram_call(): pl.pallas_call(gram_kernel, out_shape=jax.ShapeDtypeStruct((STRIP, SHARE_...]
    unnamed x19 -> x23, local copies, waits for them, and re-layouts: 7.56 us -> 10.2 us
where the time goes in v4:
time: 382 us; the launch traced here: 376 us
  Pallas kernels  320 us (84%)
  matrix products  32.9 us (9%)
  local copies, waits for them, and re-layouts  19.4 us (5%)
    pallas_call x1, Pallas kernels, scatter_call(): pl.pallas_call(functools.partial(scatter_kernel, rows), out_shape=[jax.Sh...  154 us
    pallas_call x2, Pallas kernels, gather_call(): pl.pallas_call(functools.partial(gather_kernel, Plan(len(args), items, or...  133 us
    pallas_call x1, Pallas kernels, gram_call(): pl.pallas_call(gram_kernel, out_shape=jax.ShapeDtypeStruct((STRIP, SHARE_...  24.9 us
    dot_general x3, matrix products, matmul(): return jnp.dot(left_mat, right_mat, preferred_element_type=jnp.float32)  14.2 us
    dot_general x3, matrix products, matmul_nt(): lax.dot_general(left_mat, right_mat, NT_DIMS, preferred_element_type=jnp....  14.1 us
    unnamed x23, local copies, waits for them, and re-layouts  10.2 us
    pallas_call x1, Pallas kernels, mirror_call(): pl.pallas_call(mirror_kernel, grid=(2, 4), out_shape=[full, full], in_spe...  7.82 us

profile of v4, /device:TPU:9, one launch (start us, length us, event | category | flops | bytes accessed | tf_op | source)
XLA Modules:
  0.0 376.3 jit_solution(5336569028260798102)
XLA Ops:
  0.6 0.0 copy-start
  0.6 2.8 constant_dynamic-slice_fusion.2
  3.5 0.0 copy-start.5
  3.5 2.5 copy-done
  6.0 3.4 copy-done.1
  9.4 1.2 copy-done.2
  10.6 1.2 copy-done.3
  11.9 55.2 %weights.1 = (bf16[1024,1024]{1,0:T(8,128)(2,1)S(1)}, bf16[1024,1024]{1,0:T(8,128)(2,1)S(1)}, bf16[1024,1024]{1,0:T(8,128)(2,1)S(1)}, bf16[1024,1024]{1,0:T(8,128)(2,1)S(1)}, f32[2,8,80,256]{3,2,1,0:T(8,128)S(1)}) custom-call(bf16[2,1024,256]{2,1,0:T(8,128)(2,1)S(1)} %copy-done.2, bf16[2,256,1024]{2,1,0:T(8,128)(2,1)S(1)} %copy-done.3, ...), custom_call_target="tpu_custom_call" | custom-call | flops 49999998976 | bytes 8388608 | tf_op jit(solution)/shard_map/weights/pallas_call | solution.py:389
  67.1 4.4 %fusion.18 = (bf16[1024,1024]{1,0:T(8,128)(2,1)}, bf16[1024,1024]{1,0:T(8,128)(2,1)S(1)}) fusion(bf16[1024,1024]{1,0:T(8,128)(2,1)S(1)} %get-tuple-element.51.x_ref, bf16[1024,1024]{1,0:T(8,128)(2,1)S(1)} %get-tuple-element.20), kind=kOutput, calls=%fused_computation.39 | convolution fusion | flops 2159017984 | bytes 8388608 | tf_op jit(solution)/shard_map/dot_general | solution.py:39
  71.4 4.9 %fusion.12 = (bf16[1024,1024]{1,0:T(8,128)(2,1)}, bf16[1024,1024]{1,0:T(8,128)(2,1)S(1)}) fusion(bf16[1024,1024]{1,0:T(8,128)(2,1)S(1)} %get-tuple-element.21, bf16[1024,1024]{1,0:T(8,128)(2,1)S(1)} %get-tuple-element.45), kind=kOutput, calls=%fused_computation.33 | convolution fusion | flops 2169503744 | bytes 8388608 | tf_op jit(solution)/shard_map/dot_general | solution.py:39
  76.4 4.9 %fusion.11 = (bf16[1024,1024]{1,0:T(8,128)(2,1)}, bf16[1024,1024]{1,0:T(8,128)(2,1)S(1)}) fusion(bf16[1024,1024]{1,0:T(8,128)(2,1)S(1)} %get-tuple-element.22, bf16[1024,1024]{1,0:T(8,128)(2,1)S(1)} %get-tuple-element.47), kind=kOutput, calls=%fused_computation.32 | convolution fusion | flops 2169503744 | bytes 8388608 | tf_op jit(solution)/shard_map/dot_general | solution.py:39
  81.3 4.7 %fusion.10.g3_ref = bf16[1024,1024]{1,0:T(8,128)(2,1)S(1)} fusion(bf16[1024,1024]{1,0:T(8,128)(2,1)S(1)} %get-tuple-element.49, bf16[1024,1024]{1,0:T(8,128)(2,1)S(1)} %get-tuple-element.50.dy_ref, bf16[1024,1024]{1,0:T(8,128)(2,1)S(1)} %get-tuple-element.19), kind=kOutput, calls=%fused_computation.31 | convolution fusion | flops 2170552320 | bytes 8388608 | tf_op jit(solution)/shard_map/dot_general | solution.py:47
  86.0 4.7 %fusion.17.g2_ref = bf16[1024,1024]{1,0:T(8,128)(2,1)S(1)} fusion(bf16[1024,1024]{1,0:T(8,128)(2,1)S(1)} %get-tuple-element.47, bf16[1024,1024]{1,0:T(8,128)(2,1)S(1)} %fusion.10.g3_ref, bf16[1024,1024]{1,0:T(8,128)(2,1)S(1)} %get-tuple-element.22), kind=kOutput, calls=%fused_computation.38 | convolution fusion | flops 2170552320 | bytes 8388608 | tf_op jit(solution)/shard_map/dot_general | solution.py:47
  90.7 0.0 copy-start.10
  90.7 4.7 %fusion.23.g1_ref = bf16[1024,1024]{1,0:T(8,128)(2,1)S(1)} fusion(bf16[1024,1024]{1,0:T(8,128)(2,1)S(1)} %get-tuple-element.45, bf16[1024,1024]{1,0:T(8,128)(2,1)S(1)} %fusion.17.g2_ref, bf16[1024,1024]{1,0:T(8,128)(2,1)S(1)} %get-tuple-element.21), kind=kOutput, calls=%fused_computation.44 | convolution fusion | flops 2170552320 | bytes 8388608 | tf_op jit(solution)/shard_map/dot_general | solution.py:47
  95.4 24.9 %gram.1 = f32[32,800,256]{2,1,0:T(8,128)} custom-call(bf16[1024,1024]{1,0:T(8,128)(2,1)S(1)} %get-tuple-element.51.x_ref, bf16[1024,1024]{1,0:T(8,128)(2,1)S(1)} %fusion.23.g1_ref, bf16[1024,1024]{1,0:T(8,128)(2,1)} %copy-done.10, bf16[1024,1024]{1,0:T(8,128)(2,1)} %get-tuple-element.44.h1_ref, bf16[1024,1024]{1,0:T(8,128)(2,1)} %get-tuple-element.46.h2_ref, ...), custom_call_target="tpu_custom_call" | custom-call | flops 15000000512 | bytes 46000000 | tf_op jit(solution)/shard_map/gram/pallas_call | solution.py:132
  120.3 153.9 %sums.1 = (f32[800,256]{1,0:T(8,128)}, f32[2,80,256]{2,1,0:T(8,128)}, f32[2,512,256]{2,1,0:T(8,128)}) custom-call(f32[4,2,2,2,800,256]{5,4,3,2,1,0:T(8,128)} %bitcast.51, f32[2,2,2,2,80,256]{5,4,3,2,1,0:T(8,128)} %bitcast.47), custom_call_target="tpu_custom_call" | custom-call | flops 120000004096 | bytes 62914560 | tf_op jit(solution)/shard_map/sums/pallas_call | solution.py:640
  274.3 0.0 copy-start.7
  274.3 0.0 copy-start.8
  274.3 1.4 broadcast_multiply_fusion
  275.7 4.0 %fusion.33 = f32[512,256]{1,0:T(8,128)S(1)} fusion(f32[1024,256]{1,0:T(8,128)S(1)} %bitcast.48, f32[2,1024,1024]{2,1,0:T(8,128)} %param.23, s32[]{:T(128)S(6)} %select_n.83, s32[]{:T(128)S(6)} %select_n.84, f32[2,1024,1024]{2,1,0:T(8,128)} %param.20, pred[]{:T(512)S(6)} %eq.3), kind=kOutput, calls=%fused_computation.55 | convolution fusion | flops 1611137024 | bytes 5767177 | tf_op jit(solution)/shard_map/dot_general | solution.py:51
  279.8 0.6 fusion.40.refs_1_
  280.4 0.9 slice_bitcast_fusion.2
  281.4 0.8 constant_dynamic-slice_fusion.4
  282.2 1.0 constant_dynamic-slice_fusion.6
  283.3 0.9 slice_multiply_fusion
  284.3 0.9 constant_dynamic-slice_fusion
  285.2 78.3 %results.1 = (f32[32,4,80,256]{3,2,1,0:T(8,128)S(1)}, f32[8,512,256]{2,1,0:T(8,128)S(1)}, f32[4,256,256]{2,1,0:T(8,128)S(1)}) custom-call(f32[4,80,256]{2,1,0:T(8,128)S(1)} %fusion.39.refs_0_, f32[512,256]{1,0:T(8,128)S(1)} %fusion.40.refs_1_, f32[4,32,256]{2,1,0:T(8,128)S(1)} %fusion.45.refs_2_), custom_call_target="tpu_custom_call" | custom-call | flops 49999998976 | bytes 15728640 | tf_op jit(solution)/shard_map/results/pallas_call | solution.py:389
  363.4 7.8 %mirror.1 = (f32[2,1024,1024]{2,1,0:T(8,128)}, f32[2,1024,1024]{2,1,0:T(8,128)}) custom-call(f32[4,8,4,80,256]{4,3,2,1,0:T(8,128)S(1)} %bitcast.46), custom_call_target="tpu_custom_call" | custom-call | flops 10000000000 | bytes 27262976 | tf_op jit(solution)/shard_map/mirror/pallas_call | solution.py:681
  371.3 1.7 fusion.51
  373.0 1.8 copy.23
  374.8 1.0 fusion.52
  (21 shorter events, 0.2 us)
Async XLA Ops:
  0.6 5.4 %copy-start = (bf16[4096,1024]{1,0:T(8,128)(2,1)S(1)}, bf16[4096,1024]{1,0:T(8,128)(2,1)}, u32[]{:S(2)}) copy-start(bf16[4096,1024]{1,0:T(8,128)(2,1)} %refs_3_.1) | copy-start | bytes 25165828
  3.5 77.8 %copy-start.5 = (bf16[1024,1024]{1,0:T(8,128)(2,1)}, bf16[1024,1024]{1,0:T(8,128)(2,1)S(1)}, u32[]{:S(2)}) copy-start(bf16[1024,1024]{1,0:T(8,128)(2,1)S(1)} %get-tuple-element.50.dy_ref) | copy-start | bytes 6291460
  6.0 3.4 copy-start.1
  9.4 1.2 copy-start.2
  10.6 1.2 copy-start.3
  67.0 4.4 %copy-start.4 = (f32[2,8,80,256]{3,2,1,0:T(8,128)}, f32[2,8,80,256]{3,2,1,0:T(8,128)S(1)}, u32[]{:S(2)}) copy-start(f32[2,8,80,256]{3,2,1,0:T(8,128)S(1)} %get-tuple-element.23) | copy-start | bytes 3932164
  86.0 4.7 %copy-start.9 = (bf16[1024,1024]{1,0:T(8,128)(2,1)}, bf16[1024,1024]{1,0:T(8,128)(2,1)S(1)}, u32[]{:S(2)}) copy-start(bf16[1024,1024]{1,0:T(8,128)(2,1)S(1)} %fusion.10.g3_ref) | copy-start | bytes 6291460
  90.7 4.7 %copy-start.10 = (bf16[1024,1024]{1,0:T(8,128)(2,1)}, bf16[1024,1024]{1,0:T(8,128)(2,1)S(1)}, u32[]{:S(2)}) copy-start(bf16[1024,1024]{1,0:T(8,128)(2,1)S(1)} %fusion.17.g2_ref) | copy-start | bytes 6291460
  274.3 5.5 %copy-start.7 = (f32[2,256,256]{2,1,0:T(8,128)S(1)}, f32[2,256,256]{2,1,0:T(8,128)}, u32[]{:S(2)}) copy-start(f32[2,256,256]{2,1,0:T(8,128)} %param.22) | copy-start | bytes 1572868
  274.3 5.5 %copy-start.8 = (f32[2,256,256]{2,1,0:T(8,128)S(1)}, f32[2,256,256]{2,1,0:T(8,128)}, u32[]{:S(2)}) copy-start(f32[2,256,256]{2,1,0:T(8,128)} %param.21) | copy-start | bytes 1572868
  275.7 5.7 %copy-start.6 = (f32[2,80,256]{2,1,0:T(8,128)S(1)}, f32[2,80,256]{2,1,0:T(8,128)}, u32[]{:S(2)}) copy-start(f32[2,80,256]{2,1,0:T(8,128)} %get-tuple-element.24) | copy-start | bytes 491524

commit v5 on v4

--- a/solution.py
+++ b/solution.py
@@ -97,10 +97,12 @@
             else:
                 out_copy(slot, dst).wait()
                 pltpu.make_async_copy(bstage.at[slot], out_ref.at[pl.ds(0, CORES), pl.ds(BLOCK_BASE, STRIP)], b_sem.at[slot]).wait()
-            prod = lax.dot_general(act[layer], right, TN_DIMS, preferred_element_type=jnp.float32)
-            stage[slot] = prod.reshape(2, D_ROWS, BLOCK)
+            right_t = right.T
+            prod = matmul(right_t, act[layer])
+            for q in range(4):
+                stage[slot, q // 2, pl.ds(q % 2 * BLOCK, BLOCK)] = prod[:, q * BLOCK:(q + 1) * BLOCK]
             out_copy(slot, dst).start()
-            blk = lax.dot_general(right, right, TN_DIMS, preferred_element_type=jnp.float32)
+            blk = matmul(right_t, right)
             bstage[slot] = blk.reshape(CORES, STRIP, BLOCK)
             pltpu.make_async_copy(bstage.at[slot], out_ref.at[pl.ds(m * CORES, CORES), pl.ds(BLOCK_BASE + STRIP * layer, STRIP)], b_sem.at[slot]).start()
             return carry
@@ -206,12 +208,7 @@
     n = len(plan.items)
     pieces, refs = refs[:plan.n_in], refs[plan.n_in:]
     outs, refs = refs[:n], refs[n:]
-    ends = len(plan.tokens) > 0
-    if ends:
-        ends_ref, refs = refs[0], refs[1:]
     lands, refs = refs[:n], refs[n:]
-    if ends:
-        tok, acc, tok_sem, acc_sem, *refs = refs
     load_sem, z_recv, x_recv, y_recv, d_recv, c_recv, up_send, dn_send, x_send, y_send, dy_send, dx_send, c_send, flush_sem = refs
     z, y, x, c, near = torus_place()
 
@@ -231,25 +228,6 @@
     for load in loads:
         load.start()
 
-    def tok_load(t):
-        src = pieces[plan.tokens[t // 4]].at[pl.ds(t % 4 * HIDDEN, HIDDEN)]
-        return pltpu.make_async_copy(src, tok.at[t % 2], tok_sem.at[t % 2])
-
-    def ends_out(mat):
-        return pltpu.make_async_copy(acc.at[mat], ends_ref.at[mat], acc_sem.at[mat])
-
-    def ends_step(t):
-        tok_load(t).wait()
-        put_sym(acc.at[t // 4], sym_blocks(tok.at[t % 2], z), t % 4 > 0)
-        if t + 2 < CORES:
-            tok_load(t + 2).start()
-        if t % 4 == 3:
-            ends_out(t // 4).start()
-
-    todo = list(range(CORES)) if ends else []
-    if ends:
-        tok_load(0).start()
-        tok_load(1).start()
     meet_neighbours(z, near)
 
     def side_copy(j, zs, side):
@@ -352,13 +330,6 @@
             if 0 <= step - lag < 4:
                 for j, off in waves[step - lag]:
                     func(j, off)
-                if todo:
-                    ends_step(todo.pop(0))
-    for t in todo:
-        ends_step(t)
-    if ends:
-        ends_out(0).wait()
-        ends_out(1).wait()
     for wave in waves:
         for j, off in wave:
             last_step(j, off)
@@ -370,28 +341,23 @@
 
 
 class Plan:
-    def __init__(self, n_in, items, order, tokens):
-        self.n_in, self.items, self.order, self.tokens = n_in, items, order, tokens
-
-
-def gather_call(args, items, order, collective_id, name, tokens=()):
+    def __init__(self, n_in, items, order):
+        self.n_in, self.items, self.order = n_in, items, order
+
+
+def gather_call(args, items, order, collective_id, name):
     n = len(items)
     dma = pltpu.SemaphoreType.DMA
     size = sum(math.prod(item.shape) * jnp.dtype(item.dtype).itemsize for item in items)
     hbm = pl.BlockSpec(memory_space=pltpu.HBM)
     flat = dma((n, 4))
     shapes = [jax.ShapeDtypeStruct(item.shape, item.dtype) for item in items]
-    extra = []
-    if tokens:
-        part = (2, CORES, SYM_ROWS, BLOCK)
-        shapes.append(jax.ShapeDtypeStruct(part, jnp.float32))
-        extra = [pltpu.VMEM((2, HIDDEN, HIDDEN), jnp.bfloat16), pltpu.VMEM(part, jnp.float32), dma((2,)), dma((2,))]
     return pl.pallas_call(
-        functools.partial(gather_kernel, Plan(len(args), items, order, tokens)),
+        functools.partial(gather_kernel, Plan(len(args), items, order)),
         out_shape=shapes,
         in_specs=[hbm] * len(args),
         out_specs=[hbm] * len(shapes),
-        scratch_shapes=[pltpu.VMEM(item.shape, item.dtype) for item in items] + extra
+        scratch_shapes=[pltpu.VMEM(item.shape, item.dtype) for item in items]
         + [dma((n,)), flat, flat, flat, dma((n, 4, 2)), dma((n, 4, 4)), flat, flat, flat, flat, flat, flat, dma((n, 4, 4)), dma((n, 4, CORES))],
         compiler_params=pltpu.CompilerParams(collective_id=collective_id, has_side_effects=True, vmem_limit_bytes=size + HALF_STRIP * MIB),
         cost_estimate=pl.CostEstimate(flops=50_000_000_000, bytes_accessed=size, transcendentals=0),
@@ -415,19 +381,19 @@
     return ref.at[pl.ds((zs * CORES + d) * STRIP + which * HALF_STRIP, HALF_STRIP)]
 
 
-def gather_weights(w_col, w_row, x_tokens, dy_tokens):
+def gather_weights(w_col, w_row):
     shape = (HIDDEN, HIDDEN)
     items = [Item(shape, w_col.dtype, lambda refs, z, d, i=i: refs[0].at[i, pl.ds(d * LANES, LANES)], col_slot, col_half) for i in range(2)]
     items += [Item(shape, w_row.dtype, lambda refs, z, d, i=i: refs[1].at[i, pl.ds(d * STRIP, STRIP)], row_slot, row_half) for i in range(2)]
-    return gather_call((w_col, w_row, x_tokens, dy_tokens), items, (0, 3, 2, 1), 1, 'weights', (2, 3))
+    return gather_call((w_col, w_row), items, (0, 3, 2, 1), 1, 'weights')
 
 
 def gather_results(facts, u_half, blocks):
     items = [
         Item((STRIP, 4, SYM_ROWS, BLOCK), facts.dtype, lambda refs, z, d: refs[0],
              lambda ref, zs, d: ref.at[zs * CORES + d], lambda ref, zs, d, which: ref.at[zs * CORES + d, pl.ds(2 * which, 2)]),
-        Item((CORES, D_ROWS, BLOCK), facts.dtype, lambda refs, z, d: refs[1],
-             lambda ref, zs, d: ref.at[d], lambda ref, zs, d, which: ref.at[d, pl.ds(which * BLOCK, BLOCK)], True),
+        Item((CORES, BLOCK, D_ROWS), facts.dtype, lambda refs, z, d: refs[1],
+             lambda ref, zs, d: ref.at[d], lambda ref, zs, d, which: ref.at[d, pl.ds(which * LANES, LANES)], True),
         Item((4, BLOCK, BLOCK), facts.dtype, lambda refs, z, d: refs[2],
              lambda ref, zs, d: ref.at[:, pl.ds(d * STRIP, STRIP)], lambda ref, zs, d, which: ref.at[pl.ds(2 * which, 2), pl.ds(d * STRIP, STRIP)], True),
     ]
@@ -445,14 +411,26 @@
     lax.fori_loop(0, rows // step, body, 0)
 
 
-def scatter_kernel(rows, parts_ref, ends_ref, share_ref, eshare_ref, grad_ref, own, mate, one_x, one_y, two_x, two_y, up_buf, dn_buf,
-                   eown, emate, eone, etwo, gland, e_sem, emate_sem, eone_sem, etwo_sem, g_sem, out2_sem,
+def scatter_kernel(rows, parts_ref, x_ref, dy_ref, share_ref, eshare_ref, grad_ref, own, mate, one_x, one_y, two_x, two_y, up_buf, dn_buf,
+                   tok, eacc, emate, eone, etwo, gland, e_sem, emate_sem, eone_sem, etwo_sem, g_sem, out2_sem,
                    own_sem, mate_send, mate_recv, x1_send, x1_recv, y1_send, y1_recv, x2_send, x2_recv, y2_send, y2_recv,
                    up_send, up_recv, dn_send, dn_recv, out_sem):
     z, y, x, c, near = torus_place()
     sub = rows // 4
-    eload = pltpu.make_async_copy(ends_ref.at[:, :, :, c], eown, e_sem.at[0])
-    eload.start()
+    def tok_load(t):
+        return pltpu.make_async_copy((x_ref, dy_ref)[t // 4].at[pl.ds(t % 4 * HIDDEN, HIDDEN)], tok.at[t % 2], e_sem.at[t % 2])
+
+    def ends_step(t):
+        tok_load(t).wait()
+        put_sym(eacc.at[t // 4].reshape(CORES, SYM_ROWS, BLOCK), sym_blocks(tok.at[t % 2], z), t % 4 > 0)
+        if t + 2 < CORES:
+            tok_load(t + 2).start()
+
+    def eown(mat, *where):
+        return eacc.at[(mat,) + where + (c,)]
+
+    tok_load(0).start()
+    tok_load(1).start()
     loads = {}
     for k, (zd, h) in enumerate(CHUNK_ORDER):
         loads[k] = []
@@ -462,12 +440,12 @@
             load.start()
             loads[k].append(load)
     meet_neighbours(z, near)
-    ematec = remote(ends_ref.at[:, :, :, 1 - c], emate, emate_sem.at[0], emate_sem.at[1], near['c'])
-    ematec.start()
-    eones = (remote(eown.at[0, :, 1 - x], eone.at[0], eone_sem.at[0], eone_sem.at[1], near['x']),
-             remote(eown.at[1, 1 - y], eone.at[1], eone_sem.at[2], eone_sem.at[3], near['y']))
-    etwos = (remote(eown.at[0, 1 - y, x], etwo.at[0], etwo_sem.at[0], etwo_sem.at[1], near['y']),
-             remote(eown.at[1, y, 1 - x], etwo.at[1], etwo_sem.at[2], etwo_sem.at[3], near['x']))
+    every = slice(None)
+    ematec = remote(eacc.at[:, :, :, 1 - c], emate, emate_sem.at[0], emate_sem.at[1], near['c'])
+    eones = (remote(eown(0, every, 1 - x), eone.at[0], eone_sem.at[0], eone_sem.at[1], near['x']),
+             remote(eown(1, 1 - y, every), eone.at[1], eone_sem.at[2], eone_sem.at[3], near['y']))
+    etwos = (remote(eown(0, 1 - y, x), etwo.at[0], etwo_sem.at[0], etwo_sem.at[1], near['y']),
+             remote(eown(1, y, 1 - x), etwo.at[1], etwo_sem.at[2], etwo_sem.at[3], near['x']))
     mates = {}
     for k, (zd, h) in enumerate(CHUNK_ORDER):
         mates[k] = []
@@ -562,39 +540,44 @@
                 pltpu.make_async_copy(own.at[zd, y, x, span], share_ref.at[span], out_sem.at[h, col]).start()
 
     def ends_a():
-        eload.wait()
         ematec.wait_recv()
         for mat in range(2):
             for yy in range(2):
                 for xx in range(2):
-                    add_into(eown.at[mat, yy, xx], emate.at[mat, yy, xx], SYM_ROWS)
+                    add_into(eown(mat, yy, xx), emate.at[mat, yy, xx], SYM_ROWS)
             eones[mat].start()
 
     def ends_b():
         eones[0].wait_recv()
         for yy in range(2):
-            add_into(eown.at[0, yy, x], eone.at[0, yy], SYM_ROWS)
+            add_into(eown(0, yy, x), eone.at[0, yy], SYM_ROWS)
         etwos[0].start()
         eones[1].wait_recv()
         for xx in range(2):
-            add_into(eown.at[1, y, xx], eone.at[1, xx], SYM_ROWS)
+            add_into(eown(1, y, xx), eone.at[1, xx], SYM_ROWS)
         etwos[1].start()
 
     def ends_c():
         for mat in range(2):
             etwos[mat].wait_recv()
-            add_into(eown.at[mat, y, x], etwo.at[mat], SYM_ROWS)
-            pltpu.make_async_copy(eown.at[mat, y, x], eshare_ref.at[mat], out2_sem.at[mat]).start()
+            add_into(eown(mat, y, x), etwo.at[mat], SYM_ROWS)
+            pltpu.make_async_copy(eown(mat, y, x), eshare_ref.at[mat], out2_sem.at[mat]).start()
 
     n = len(CHUNK_ORDER)
-    ends_a()
     for step in range(n + 3):
-        if step == 1:
-            ends_b()
-        if step == 2:
-            ends_c()
         if step < n:
             step_a(step)
+        if step < 4:
+            ends_step(2 * step)
+            ends_step(2 * step + 1)
+        if step == 4:
+            ematec.start()
+        if step == 5:
+            ends_a()
+        if step == 6:
+            ends_b()
+        if step == CORES:
+            ends_c()
         if 0 <= step - 1 < n:
             step_b(step - 1)
         if 0 <= step - 3 < n:
@@ -620,12 +603,12 @@
             span = spans(h)[col]
             pltpu.make_async_copy(own.at[0, y, x, span], share_ref.at[span], out_sem.at[h, col]).wait()
     for mat in range(2):
-        pltpu.make_async_copy(eown.at[mat, y, x], eshare_ref.at[mat], out2_sem.at[mat]).wait()
+        pltpu.make_async_copy(eown(mat, y, x), eshare_ref.at[mat], out2_sem.at[mat]).wait()
     gout.wait()
     gmate.wait()
 
 
-def scatter_call(parts, ends, collective_id, name):
+def scatter_call(parts, x_tokens, dy_tokens, collective_id, name):
     rows = parts.shape[-2]
     half = rows // 2
     f32 = jnp.float32
@@ -635,21 +618,20 @@
     one_buf = pltpu.VMEM((4, 2, half, BLOCK), f32)
     two_buf = pltpu.VMEM((4, half, BLOCK), f32)
     z_buf = pltpu.VMEM((4, rows, BLOCK), f32)
-    e_buf = pltpu.VMEM((2, 2, 2, SYM_ROWS, BLOCK), f32)
     hbm = pl.BlockSpec(memory_space=pltpu.HBM)
     return pl.pallas_call(
         functools.partial(scatter_kernel, rows),
         out_shape=[jax.ShapeDtypeStruct((rows, BLOCK), f32), jax.ShapeDtypeStruct((2, SYM_ROWS, BLOCK), f32), jax.ShapeDtypeStruct((2, D_ROWS, BLOCK), f32)],
-        in_specs=[hbm] * 2,
+        in_specs=[hbm] * 3,
         out_specs=[hbm] * 3,
         scratch_shapes=[whole, whole, one_buf, one_buf, two_buf, two_buf, z_buf, z_buf,
-                        e_buf, e_buf, pltpu.VMEM((2, 2, SYM_ROWS, BLOCK), f32), pltpu.VMEM((2, SYM_ROWS, BLOCK), f32), pltpu.VMEM((D_ROWS, BLOCK), f32),
-                        dma((1,)), dma((2,)), dma((4,)), dma((4,)), dma((2,)), dma((4,))]
+                        pltpu.VMEM((2, HIDDEN, HIDDEN), x_tokens.dtype), pltpu.VMEM((2, 2, 2, 2, SYM_ROWS, BLOCK), f32), pltpu.VMEM((2, 2, 2, SYM_ROWS, BLOCK), f32), pltpu.VMEM((2, 2, SYM_ROWS, BLOCK), f32), pltpu.VMEM((2, SYM_ROWS, BLOCK), f32), pltpu.VMEM((D_ROWS, BLOCK), f32),
+                        dma((2,)), dma((2,)), dma((4,)), dma((4,)), dma((2,)), dma((4,))]
         + [dma((n, 2))] * 3 + [dma((n,))] * CORES + [dma((n, 2))] * 4 + [dma((2, 2))],
         compiler_params=pltpu.CompilerParams(collective_id=collective_id, has_side_effects=True, vmem_limit_bytes=60 * MIB),
         cost_estimate=pl.CostEstimate(flops=120_000_000_000, bytes_accessed=60 * MIB, transcendentals=0),
         name=name,
-    )(parts.reshape(4, 2, 2, 2, rows, BLOCK), ends.reshape(2, 2, 2, 2, SYM_ROWS, BLOCK))
+    )(parts.reshape(4, 2, 2, 2, rows, BLOCK), x_tokens, dy_tokens)
 
 
 def mirror_kernel(in_ref, a_ref, s_ref):
@@ -698,7 +680,7 @@
         model_id = lax.axis_index('model')
         data_id = lax.axis_index('data')
         inv_rows = 1.0 / (x_tokens.shape[0] * data_ways)
-        w_one, w_three, w_two, w_four, ends = gather_weights(w_col, w_row, x_tokens, dy_tokens)
+        w_one, w_three, w_two, w_four = gather_weights(w_col, w_row)
         rows_dev = x_tokens.shape[0] // model_ways
         x_loc = lax.dynamic_slice(x_tokens, (rows_dev * model_id, 0), (rows_dev, HIDDEN))
         dy_loc = lax.dynamic_slice(dy_tokens, (rows_dev * model_id, 0), (rows_dev, HIDDEN))
@@ -712,7 +694,7 @@
         g_two = back_gate(matmul_nt(g_three, w_three).astype(jnp.bfloat16), z_two)
         g_one = back_gate(matmul_nt(g_two, w_two).astype(jnp.bfloat16), z_one)
         parts = gram_call(x_loc, g_one, g_two, h_one, h_two, g_three, dy_loc, h_three)
-        share, eshare, grad_mat = scatter_call(parts, ends, 2, 'sums')
+        share, eshare, grad_mat = scatter_call(parts, x_tokens, dy_tokens, 2, 'sums')
         keep = 1.0 - FACTOR_DECAY
         low = lax.rem(model_id, 2)
         spots = ((model_id * BLOCK + STRIP * data_id, model_id * BLOCK, STRIP),
@@ -722,22 +704,22 @@
         mids = share[FULL_BASE:BLOCK_BASE].reshape(2, SYM_ROWS, BLOCK)
         sums = jnp.stack([eshare[0], mids[1], mids[0], eshare[1]])
         facts = FACTOR_DECAY * jnp.stack(olds, axis=1).reshape(4, SYM_ROWS, BLOCK) + keep * inv_rows * sums
-        grad_mat = grad_mat.reshape(HIDDEN, BLOCK) * inv_rows
+        grad_mat = jnp.swapaxes(grad_mat.reshape(4, BLOCK, BLOCK), 0, 1).reshape(BLOCK, HIDDEN) * inv_rows
         layer_id = data_id // 2
         stack_id = layer_id // 2
         is_col = lax.rem(layer_id, 2) == 0
         half_at = lax.rem(data_id, 2) * D_ROWS
         full_inv = jnp.where(is_col, *[lax.dynamic_slice(inv, (stack_id, half_at, 0), (1, D_ROWS, HIDDEN))[0] for inv in (a_inv_col, s_inv_row)])
         block_inv = jnp.where(is_col, *[lax.dynamic_slice(inv, (stack_id, 0, 0), (1, BLOCK, BLOCK))[0] for inv in (s_inv_col, a_inv_row)])
-        u_half = exact_dot(exact_dot(full_inv, grad_mat), block_inv)
+        u_half = lax.dot_general(exact_dot(block_inv, grad_mat), full_inv, NT_DIMS, precision=EXACT, preferred_element_type=jnp.float32)
         old_blocks = jnp.concatenate([lax.dynamic_slice(old, (0, STRIP * data_id, 0), (2, STRIP, BLOCK)) for old in (s_old_col, a_old_row)])
         new_blocks = jnp.swapaxes(share[BLOCK_BASE:].reshape(2, 2, STRIP, BLOCK), 0, 1).reshape(4, STRIP, BLOCK)
         blocks = FACTOR_DECAY * old_blocks + keep * inv_rows * new_blocks
         fact_all, u_all, blk_all = gather_results(facts, u_half, blocks)
         a_new_col, s_new_row = mirror_call(fact_all)
-        u_all = u_all.reshape(2, 2, HIDDEN, BLOCK)
-        u_col = u_all[:, 0]
-        u_row = jnp.swapaxes(u_all[:, 1], 1, 2)
+        u_all = u_all.reshape(2, 2, 2, BLOCK, D_ROWS)
+        u_col = jnp.transpose(u_all[:, 0], (0, 1, 3, 2)).reshape(2, HIDDEN, BLOCK)
+        u_row = jnp.swapaxes(u_all[:, 1], 1, 2).reshape(2, BLOCK, HIDDEN)
         return (u_col, u_row, a_new_col, blk_all[:2], blk_all[2:], s_new_row)
 
     batch_split = P('data', None)

time: 382 us -> 380 us (level)
  the two profiles are of different devices: /device:TPU:9 before, /device:TPU:11 now
where the time goes in v5:
time: 380 us; the launch traced here: 373 us
  Pallas kernels  322 us (85%)
  matrix products  33.7 us (9%)
  local copies, waits for them, and re-layouts  14.3 us (4%)
    pallas_call x1, Pallas kernels, scatter_call(): pl.pallas_call(functools.partial(scatter_kernel, rows), out_shape=[jax.Sh...  162 us
    pallas_call x2, Pallas kernels, gather_call(): pl.pallas_call(functools.partial(gather_kernel, Plan(len(args), items, or...  128 us
    pallas_call x1, Pallas kernels, gram_call(): pl.pallas_call(gram_kernel, out_shape=jax.ShapeDtypeStruct((STRIP, SHARE_...  24.7 us
    dot_general x3, matrix products, matmul(): return jnp.dot(left_mat, right_mat, preferred_element_type=jnp.float32)  14.4 us
    dot_general x3, matrix products, matmul_nt(): lax.dot_general(left_mat, right_mat, NT_DIMS, preferred_element_type=jnp....  14.1 us
    pallas_call x1, Pallas kernels, mirror_call(): pl.pallas_call(mirror_kernel, grid=(2, 4), out_shape=[full, full], in_spe...  7.82 us

profile of v5, /device:TPU:11, one launch (start us, length us, event | category | flops | bytes accessed | tf_op | source)
XLA Modules:
  0.0 373.5 jit_solution(17814545015089700509)
XLA Ops:
  0.7 2.8 constant_dynamic-slice_fusion.2
  3.5 0.0 copy-start.2
  3.5 0.0 copy-done
  3.5 0.0 copy-done.1
  3.5 43.9 %weights.1 = (bf16[1024,1024]{1,0:T(8,128)(2,1)S(1)}, bf16[1024,1024]{1,0:T(8,128)(2,1)S(1)}, bf16[1024,1024]{1,0:T(8,128)(2,1)S(1)}, bf16[1024,1024]{1,0:T(8,128)(2,1)S(1)}) custom-call(bf16[2,1024,256]{2,1,0:T(8,128)(2,1)S(1)} %copy-done, bf16[2,256,1024]{2,1,0:T(8,128)(2,1)S(1)} %copy-done.1), custom_call_target="tpu_custom_call" | custom-call | flops 49999998976 | bytes 8388608 | tf_op jit(solution)/shard_map/weights/pallas_call | solution.py:355
  47.4 4.4 %fusion.18 = (bf16[1024,1024]{1,0:T(8,128)(2,1)}, bf16[1024,1024]{1,0:T(8,128)(2,1)S(1)}) fusion(bf16[1024,1024]{1,0:T(8,128)(2,1)S(1)} %get-tuple-element.49.x_ref, bf16[1024,1024]{1,0:T(8,128)(2,1)S(1)} %get-tuple-element.19), kind=kOutput, calls=%fused_computation.39 | convolution fusion | flops 2159017984 | bytes 8388608 | tf_op jit(solution)/shard_map/dot_general | solution.py:39
  51.8 5.1 %fusion.12 = (bf16[1024,1024]{1,0:T(8,128)(2,1)}, bf16[1024,1024]{1,0:T(8,128)(2,1)S(1)}) fusion(bf16[1024,1024]{1,0:T(8,128)(2,1)S(1)} %get-tuple-element.20, bf16[1024,1024]{1,0:T(8,128)(2,1)S(1)} %get-tuple-element.43), kind=kOutput, calls=%fused_computation.33 | convolution fusion | flops 2169503744 | bytes 8388608 | tf_op jit(solution)/shard_map/dot_general | solution.py:39
  56.8 4.9 %fusion.11 = (bf16[1024,1024]{1,0:T(8,128)(2,1)}, bf16[1024,1024]{1,0:T(8,128)(2,1)S(1)}) fusion(bf16[1024,1024]{1,0:T(8,128)(2,1)S(1)} %get-tuple-element.21, bf16[1024,1024]{1,0:T(8,128)(2,1)S(1)} %get-tuple-element.45), kind=kOutput, calls=%fused_computation.32 | convolution fusion | flops 2169503744 | bytes 8388608 | tf_op jit(solution)/shard_map/dot_general | solution.py:39
  61.8 4.7 %fusion.10.g3_ref = bf16[1024,1024]{1,0:T(8,128)(2,1)S(1)} fusion(bf16[1024,1024]{1,0:T(8,128)(2,1)S(1)} %get-tuple-element.47, bf16[1024,1024]{1,0:T(8,128)(2,1)S(1)} %get-tuple-element.48.dy_ref, bf16[1024,1024]{1,0:T(8,128)(2,1)S(1)} %get-tuple-element.18), kind=kOutput, calls=%fused_computation.31 | convolution fusion | flops 2170552320 | bytes 8388608 | tf_op jit(solution)/shard_map/dot_general | solution.py:47
  66.5 4.7 %fusion.17.g2_ref = bf16[1024,1024]{1,0:T(8,128)(2,1)S(1)} fusion(bf16[1024,1024]{1,0:T(8,128)(2,1)S(1)} %get-tuple-element.45, bf16[1024,1024]{1,0:T(8,128)(2,1)S(1)} %fusion.10.g3_ref, bf16[1024,1024]{1,0:T(8,128)(2,1)S(1)} %get-tuple-element.21), kind=kOutput, calls=%fused_computation.38 | convolution fusion | flops 2170552320 | bytes 8388608 | tf_op jit(solution)/shard_map/dot_general | solution.py:47
  71.2 0.0 copy-start.7
  71.2 4.7 %fusion.23.g1_ref = bf16[1024,1024]{1,0:T(8,128)(2,1)S(1)} fusion(bf16[1024,1024]{1,0:T(8,128)(2,1)S(1)} %get-tuple-element.43, bf16[1024,1024]{1,0:T(8,128)(2,1)S(1)} %fusion.17.g2_ref, bf16[1024,1024]{1,0:T(8,128)(2,1)S(1)} %get-tuple-element.20), kind=kOutput, calls=%fused_computation.44 | convolution fusion | flops 2170552320 | bytes 8388608 | tf_op jit(solution)/shard_map/dot_general | solution.py:47
  75.9 24.7 %gram.1 = f32[32,800,256]{2,1,0:T(8,128)} custom-call(bf16[1024,1024]{1,0:T(8,128)(2,1)S(1)} %get-tuple-element.49.x_ref, bf16[1024,1024]{1,0:T(8,128)(2,1)S(1)} %fusion.23.g1_ref, bf16[1024,1024]{1,0:T(8,128)(2,1)} %copy-done.7, bf16[1024,1024]{1,0:T(8,128)(2,1)} %get-tuple-element.42.h1_ref, bf16[1024,1024]{1,0:T(8,128)(2,1)} %get-tuple-element.44.h2_ref, ...), custom_call_target="tpu_custom_call" | custom-call | flops 15000000512 | bytes 46000000 | tf_op jit(solution)/shard_map/gram/pallas_call | solution.py:134
  100.7 161.5 %sums.1 = (f32[800,256]{1,0:T(8,128)}, f32[2,80,256]{2,1,0:T(8,128)}, f32[2,512,256]{2,1,0:T(8,128)}) custom-call(f32[4,2,2,2,800,256]{5,4,3,2,1,0:T(8,128)} %bitcast.58, bf16[4096,1024]{1,0:T(8,128)(2,1)} %x_ref.1, bf16[4096,1024]{1,0:T(8,128)(2,1)} %dy_ref.1), custom_call_target="tpu_custom_call" | custom-call | flops 120000004096 | bytes 62914560 | tf_op jit(solution)/shard_map/sums/pallas_call | solution.py:622
  262.2 0.0 copy-start.4
  262.2 0.0 copy-start.5
  262.2 1.4 broadcast_multiply_fusion
  263.6 0.3 copy.23
  264.0 0.0 copy-done.4
  264.0 1.0 fusion.40
  265.0 4.2 %fusion.33.refs_1_ = f32[256,512]{1,0:T(8,128)S(1)} fusion(f32[256,1024]{1,0:T(8,128)S(1)} %fusion.40, f32[2,1024,1024]{2,1,0:T(8,128)} %param.23, s32[]{:T(128)S(6)} %select_n.83, s32[]{:T(128)S(6)} %select_n.87, f32[2,1024,1024]{2,1,0:T(8,128)} %param.20, pred[]{:T(512)S(6)} %eq.3), kind=kOutput, calls=%fused_computation.56 | convolution fusion | flops 1611137024 | bytes 5767177 | tf_op jit(solution)/shard_map/dot_general | solution.py:714
  269.3 0.9 slice_bitcast_fusion.3
  270.3 0.8 constant_dynamic-slice_fusion.4
  271.1 1.0 constant_dynamic-slice_fusion.6
  272.2 0.9 slice_multiply_fusion
  273.1 0.9 constant_dynamic-slice_fusion
  274.1 83.7 %results.1 = (f32[32,4,80,256]{3,2,1,0:T(8,128)S(1)}, f32[8,256,512]{2,1,0:T(8,128)S(1)}, f32[4,256,256]{2,1,0:T(8,128)S(1)}) custom-call(f32[4,80,256]{2,1,0:T(8,128)S(1)} %fusion.39.refs_0_, f32[256,512]{1,0:T(8,128)S(1)} %fusion.33.refs_1_, f32[4,32,256]{2,1,0:T(8,128)S(1)} %fusion.45.refs_2_), custom_call_target="tpu_custom_call" | custom-call | flops 49999998976 | bytes 15728640 | tf_op jit(solution)/shard_map/results/pallas_call | solution.py:355
  357.8 7.8 %mirror.1 = (f32[2,1024,1024]{2,1,0:T(8,128)}, f32[2,1024,1024]{2,1,0:T(8,128)}) custom-call(f32[4,8,4,80,256]{4,3,2,1,0:T(8,128)S(1)} %bitcast.52), custom_call_target="tpu_custom_call" | custom-call | flops 10000000000 | bytes 27262976 | tf_op jit(solution)/shard_map/mirror/pallas_call | solution.py:663
  365.6 2.0 slice_bitcast_fusion
  367.5 2.9 copy.25
  370.4 1.6 copy.27
  372.0 1.0 fusion.51
  (17 shorter events, 0.2 us)
Async XLA Ops:
  0.6 2.8 copy-start
  0.6 2.8 copy-start.1
  3.5 58.3 %copy-start.2 = (bf16[1024,1024]{1,0:T(8,128)(2,1)}, bf16[1024,1024]{1,0:T(8,128)(2,1)S(1)}, u32[]{:S(2)}) copy-start(bf16[1024,1024]{1,0:T(8,128)(2,1)S(1)} %get-tuple-element.48.dy_ref) | copy-start | bytes 6291460
  66.4 4.7 %copy-start.6 = (bf16[1024,1024]{1,0:T(8,128)(2,1)}, bf16[1024,1024]{1,0:T(8,128)(2,1)S(1)}, u32[]{:S(2)}) copy-start(bf16[1024,1024]{1,0:T(8,128)(2,1)S(1)} %fusion.10.g3_ref) | copy-start | bytes 6291460
  71.2 4.7 %copy-start.7 = (bf16[1024,1024]{1,0:T(8,128)(2,1)}, bf16[1024,1024]{1,0:T(8,128)(2,1)S(1)}, u32[]{:S(2)}) copy-start(bf16[1024,1024]{1,0:T(8,128)(2,1)S(1)} %fusion.17.g2_ref) | copy-start | bytes 6291460
  262.2 1.8 copy-start.4
  262.2 1.8 copy-start.5
  264.0 6.2 %copy-start.3 = (f32[2,80,256]{2,1,0:T(8,128)S(1)}, f32[2,80,256]{2,1,0:T(8,128)}, u32[]{:S(2)}) copy-start(f32[2,80,256]{2,1,0:T(8,128)} %get-tuple-element.22) | copy-start | bytes 491524
